TPU v7x, 32 devices: a whole 2x2x4 slice. The times are simulated.
32 devices in a mesh: seq: 2 (over y), section: 4 (over x, core), tp: 4 (over z).
Axes of the slice: x: 2, y: 2, z: 4, core: 2. Of those that a mesh axis runs over, the one named last changes fastest.
Arguments:
- token_ids: int32 [128], P('seq'), may hold values from 0 to 65535
- embed_columns: bfloat16 [4096, 65536], P(('tp', 'seq')), may hold values from -6 to 6
- norm_gain: bfloat16 [4, 4096], P('section'), may hold values from 0.099609375 to 1.8984375
- qkv_weight: bfloat16 [4, 4096, 4096], P('section', 'seq', 'tp'), may hold values from -1 to 1
- out_weight: bfloat16 [4, 4096, 2048], P('section', 'seq', 'tp'), may hold values from -0.125 to 0.125
Outputs:
- layer_states: bfloat16 [4, 128, 4096], P('section', 'seq', 'tp')
All inputs are finite; a program needn't handle non-finite values.
Results may differ from a plain program's by a relative error of at most 0.02.
Values may be sent and summed in bfloat16 or wider, within the bound.
No kernel may reach another device: no remote copies, remote signals or barrier semaphores. Data moves between devices by JAX's collectives and lax.ppermute only.
A program may use at most 192 MiB of HBM per device.

v0:
```python
import functools

import jax
import jax.numpy as jnp
import numpy as np
from jax import lax
from jax.experimental import pallas as pl
from jax.experimental.pallas import tpu as pltpu
from jax.sharding import PartitionSpec as P


QUERY_HEADS = 16
KEY_VALUE_HEADS = 8
HEAD_WIDTH = 128

EPS = 1e-05
ROPE_BASE = 500000.0
MASKED = -1e30
LANES = 128
AXES = ("seq", "section", "tp")


def rope_tables(positions, head_size):
    half_width = head_size // 2
    inverse_freq = ROPE_BASE ** (-jnp.arange(half_width).astype(jnp.float32) * (2.0 / head_size))
    angles = positions.astype(jnp.float32)[:, None] * inverse_freq[None, :]
    return (jnp.cos(angles), jnp.sin(angles))


def full_rope_tables(count, head_size):
    half_width = head_size // 2
    exponents = -np.arange(half_width).astype(np.float32) * np.float32(2.0 / head_size)
    inverse_freq = np.float32(ROPE_BASE) ** exponents
    angles = np.arange(count).astype(np.float32)[:, None] * inverse_freq[None, :]
    cosine, sine = np.cos(angles), np.sin(angles)
    return (
        np.concatenate([cosine, cosine], axis=1).astype(np.float32),
        np.concatenate([-sine, sine], axis=1).astype(np.float32),
    )


VMEM = pl.BlockSpec(memory_space=pltpu.VMEM)
SMEM = pl.BlockSpec(memory_space=pltpu.SMEM)
ANY = pl.BlockSpec(memory_space=pl.ANY)
HBM = pl.BlockSpec(memory_space=pltpu.HBM)


def on_section(kernel, section):
    def gated(*refs):
        pl.when(lax.axis_index("section") == section)(lambda: kernel(*refs))

    return gated


def lookup_kernel(ids_smem, ids_row, table, out, strips, onehot, sems):
    @pl.when(lax.axis_index("section") > 0)
    def _():
        read_columns(ids_smem, ids_row, table, out, strips, onehot, sems)


def read_columns(ids_smem, ids_row, table, out, strips, onehot, sems):
    features, _ = table.shape
    count = ids_row.shape[1]

    def start(i, _):
        first = pl.multiple_of((ids_smem[i] // LANES) * LANES, LANES)
        pltpu.make_async_copy(
            table.at[:, pl.ds(first, LANES)],
            strips.at[:, pl.ds(pl.multiple_of(i * LANES, LANES), LANES)],
            sems.at[i],
        ).start()
        return 0

    lax.fori_loop(0, count, start, 0)
    lanes = lax.rem(ids_row[...], LANES)
    group = 8
    acc = jnp.zeros((features, count), jnp.float32)
    wide = group * LANES
    rows = lax.broadcasted_iota(jnp.int32, (wide, count), 0)
    target = lax.broadcasted_iota(jnp.int32, (1, count), 1) * LANES + lanes
    for g in range(count // group):
        onehot[g] = jnp.where(rows + g * wide == target, 1.0, 0.0).astype(jnp.bfloat16)
    for g in range(count // group):
        for i in range(g * group, (g + 1) * group):
            pltpu.make_async_copy(
                table.at[:, pl.ds(0, LANES)],
                strips.at[:, pl.ds(i * LANES, LANES)],
                sems.at[i],
            ).wait()
        acc = acc + jnp.dot(
            strips[:, g * wide : (g + 1) * wide], onehot[g], preferred_element_type=jnp.float32
        )
    out[...] = acc.T.astype(jnp.bfloat16)


def lookup(ids, table):
    count, features = ids.shape[0], table.shape[0]
    return pl.pallas_call(
        lookup_kernel,
        out_shape=jax.ShapeDtypeStruct((count, features), jnp.bfloat16),
        in_specs=[SMEM, VMEM, ANY],
        out_specs=VMEM,
        scratch_shapes=[
            pltpu.VMEM((features, count * LANES), jnp.bfloat16),
            pltpu.VMEM((count // 8, 8 * LANES, count), jnp.bfloat16),
            pltpu.SemaphoreType.DMA((count,)),
        ],
        name="lookup",
        compiler_params=pltpu.CompilerParams(vmem_limit_bytes=16 << 20),
    )(ids, ids.reshape(1, count), table)


def send_order(ways):
    return sorted(range(ways), key=lambda k: -min(k, ways - k))


def whole_piece(rank, k, ways, parts):
    if len(parts) == 1:
        return parts[0][...]
    even = lax.rem(rank + ways - k, 2) == 0
    first, second = parts[0][...], parts[1][...]
    return jnp.concatenate([jnp.where(even, first, second), jnp.where(even, second, first)], axis=0)


def project_kernel(*refs, ways, split, last):
    pieces, (gain, weight, message, *kept) = refs[: ways * split], refs[ways * split :]
    rank, group = lax.axis_index("tp"), lax.axis_index("seq")
    width = pieces[0].shape[1]
    squares = None
    acc = None
    for n, k in enumerate(send_order(ways)):
        piece = whole_piece(rank, k, ways, pieces[n * split : (n + 1) * split])
        if last:
            kept[2][:, pl.ds(pl.multiple_of(lax.rem(rank + ways - k, ways) * width, width), width)] = piece
        elif k == 0:
            kept[0][...] = piece
        values = piece.astype(jnp.float32)
        square = jnp.sum(values * values, axis=1, keepdims=True)
        squares = square if squares is None else squares + square
        first = pl.multiple_of(lax.rem(rank + ways - k, ways) * width, width)
        scaled = (values * gain[:, pl.ds(first, width)]).astype(jnp.bfloat16)
        part = jnp.dot(scaled, weight[0, pl.ds(first, width), :], preferred_element_type=jnp.float32)
        acc = part if acc is None else acc + part
    cols = acc.shape[1]
    message[:, :cols] = acc.astype(jnp.bfloat16)
    high = squares.astype(jnp.bfloat16)
    low = squares - high.astype(jnp.float32)
    lane = lax.broadcasted_iota(jnp.int32, (acc.shape[0], LANES), 1)
    message[:, cols:] = jnp.where(lane < LANES // 2, high.astype(jnp.float32), low).astype(jnp.bfloat16)
    if last:
        mine, other, whole = kept
        block, quarter = mine.shape
        first = pl.multiple_of(lax.rem(rank, 2) * quarter, quarter)
        mine[...] = whole[pl.ds(pl.multiple_of(group * block, block), block), pl.ds(first, quarter)]
        other[...] = whole[pl.ds(pl.multiple_of((1 - group) * block, block), block), pl.ds(first, quarter)]


def project(section, pieces, gain, weight, ways, last):
    split = len(pieces) // ways
    rows, width = pieces[0].shape[0] * split, pieces[0].shape[1]
    cols = weight.shape[2]
    kept = [(rows // 2, 2 * width)] * 2 if last else [(rows, width)]
    return pl.pallas_call(
        on_section(functools.partial(project_kernel, ways=ways, split=split, last=last), section),
        out_shape=[
            jax.ShapeDtypeStruct((rows, cols + LANES), jnp.bfloat16),
        ]
        + [jax.ShapeDtypeStruct(shape, jnp.bfloat16) for shape in kept],
        in_specs=[VMEM] * (len(pieces) + 2),
        out_specs=[VMEM] * (1 + len(kept)),
        scratch_shapes=[pltpu.VMEM((rows, ways * width), jnp.bfloat16)] if last else [],
        name="project",
        compiler_params=pltpu.CompilerParams(vmem_limit_bytes=6 << 20),
    )(*pieces, gain, weight)


def stage_kernel(weight, after, out, sem, *, section):
    def bring():
        copy = pltpu.make_async_copy(weight, out, sem)
        copy.start()
        copy.wait()

    if section is None:
        bring()
    else:
        pl.when(lax.axis_index("section") == section)(bring)


def stage(weight, after, section=None):
    return pl.pallas_call(
        functools.partial(stage_kernel, section=section),
        out_shape=jax.ShapeDtypeStruct(weight.shape, weight.dtype),
        in_specs=[ANY if section is None else HBM, ANY],
        out_specs=VMEM,
        scratch_shapes=[pltpu.SemaphoreType.DMA],
        name="stage",
        compiler_params=pltpu.CompilerParams(vmem_limit_bytes=1 << 20),
    )(weight, after)


def attended_heads(total, inverse, cosine, sine, block, query_heads, key_value_heads, only):
    rows = total.shape[0]
    asked = rows if only is None else block
    repeat = query_heads // key_value_heads

    def head(i):
        return total[:, i * HEAD_WIDTH : (i + 1) * HEAD_WIDTH] * inverse

    def chosen(values):
        if only is None:
            return values
        blocks = [values[i * block : (i + 1) * block] for i in range(rows // block)]
        picked = blocks[0]
        for i in range(1, len(blocks)):
            picked = jnp.where(only == i, blocks[i], picked)
        return picked

    def rotated(i, pick=lambda values: values):
        values = pick(head(i))
        turned = values * pick(cosine) + pltpu.roll(values, HEAD_WIDTH // 2, 1) * pick(sine)
        return turned.astype(jnp.bfloat16)

    row = lax.broadcasted_iota(jnp.int32, (asked, rows), 0)
    row = row if only is None else row + only * block
    col = lax.broadcasted_iota(jnp.int32, (asked, rows), 1)
    row_block, col_block = row // block, col // block
    allowed = ((row_block == col_block) & (col <= row)) | ((col_block == 0) & (row_block > 0))
    keys = [rotated(query_heads + j) for j in range(key_value_heads)]
    held = [head(query_heads + key_value_heads + j).astype(jnp.bfloat16) for j in range(key_value_heads)]
    results = []
    for i in range(query_heads):
        scores = lax.dot_general(
            rotated(i, chosen), keys[i // repeat], (((1,), (1,)), ((), ())), preferred_element_type=jnp.float32
        ) * HEAD_WIDTH ** (-0.5)
        scores = jnp.where(allowed, scores, MASKED)
        top = jnp.max(scores, axis=1, keepdims=True)
        powers = jnp.exp(scores - top)
        weights = (powers / jnp.sum(powers, axis=1, keepdims=True)).astype(jnp.bfloat16)
        results.append(
            jnp.dot(weights, held[i // repeat], preferred_element_type=jnp.float32).astype(jnp.bfloat16)
        )
    return jnp.concatenate(results, axis=1)


def summed(got, mine, features):
    cols = mine.shape[1] - LANES
    squares = sum(
        message[:, at : at + 1].astype(jnp.float32) for message in (got, mine) for at in (cols, cols + LANES // 2)
    )
    inverse = lax.rsqrt(squares / features + EPS)
    return mine[:, :cols].astype(jnp.float32) + got[:, :cols].astype(jnp.float32), inverse


def times_transposed(left, right):
    return lax.dot_general(left, right, (((1,), (1,)), ((), ())), preferred_element_type=jnp.float32)


def attend_kernel(got, mine, cosine, sine, lent, *refs, ways, block, features, heads):
    outs, (weight, sem) = refs[:ways], refs[ways:]
    copy = pltpu.make_async_copy(lent, weight, sem)
    copy.start()
    rank = lax.axis_index("tp")
    width = weight.shape[1] // ways
    total, inverse = summed(got, mine, features)
    attended = attended_heads(total, inverse, cosine[...], sine[...], block, *heads, None)
    copy.wait()
    for k in range(ways):
        first = pl.multiple_of(lax.rem(rank + k, ways) * width, width)
        outs[k][...] = times_transposed(attended, weight[0, pl.ds(first, width), :]).astype(outs[k].dtype)


def last_kernel(got, mine, cosine, sine, lent, far_weight, *refs, ways, block, features, heads):
    outs, (weight, sem, other_weight, other_sem, slots) = refs[:ways], refs[ways:]
    rank, group = lax.axis_index("tp"), lax.axis_index("seq")
    width = outs[0].shape[1]
    copies = [
        pltpu.make_async_copy(lent, weight, sem),
        pltpu.make_async_copy(far_weight, other_weight, other_sem),
    ]
    for copy in copies:
        copy.start()
    total, inverse = summed(got, mine, features)
    attended = attended_heads(total, inverse, cosine[...], sine[...], block, *heads, group)
    per_half = weight.shape[1] // width
    for side, held, copy in ((group, weight, copies[0]), (1 - group, other_weight, copies[1])):
        copy.wait()
        for i in range(per_half):
            shift = lax.rem(side * per_half + i + ways - rank, ways)
            product = times_transposed(attended, held[0, i * width : (i + 1) * width, :])
            slots[shift] = product.astype(slots.dtype)
    for k in range(ways):
        outs[k][...] = slots[k]


def attend(section, got, mine, cosine, sine, weights, ways, block, features, heads):
    last = len(weights) > 1
    shape = (block, features // ways) if last else (mine.shape[0], weights[0].shape[1] // ways)
    return pl.pallas_call(
        on_section(
            functools.partial(
                last_kernel if last else attend_kernel, ways=ways, block=block, features=features, heads=heads
            ),
            section,
        ),
        out_shape=[jax.ShapeDtypeStruct(shape, jnp.bfloat16) for _ in range(ways)],
        in_specs=[VMEM] * 4 + [HBM] * len(weights),
        out_specs=[VMEM] * ways,
        scratch_shapes=[
            scratch
            for weight in weights
            for scratch in (pltpu.VMEM(weight.shape, jnp.bfloat16), pltpu.SemaphoreType.DMA)
        ]
        + ([pltpu.VMEM((ways,) + shape, jnp.bfloat16)] if last else []),
        name="attend",
        compiler_params=pltpu.CompilerParams(vmem_limit_bytes=8 << 20),
    )(got, mine, cosine, sine, *weights)


def combine_kernel(*refs, ways):
    parts, (residual, out) = refs[:ways], refs[ways:]
    total = parts[0][...].astype(jnp.float32)
    for part in parts[1:]:
        total = total + part[...].astype(jnp.float32)
    out[...] = (residual[...].astype(jnp.float32) + total).astype(jnp.bfloat16)


def combine(parts, residual):
    return pl.pallas_call(
        functools.partial(combine_kernel, ways=len(parts)),
        out_shape=jax.ShapeDtypeStruct(residual.shape, jnp.bfloat16),
        in_specs=[VMEM] * (len(parts) + 1),
        out_specs=VMEM,
        name="combine",
        compiler_params=pltpu.CompilerParams(vmem_limit_bytes=4 << 20),
    )(*parts, residual)


def finish_kernel(*refs, ways):
    parts, (residual, third, first, second, out) = refs[:ways], refs[ways:]
    group, section = lax.axis_index("seq"), lax.axis_index("section")
    sections = lax.axis_size("section")
    width = first.shape[1]

    @pl.when(section == sections - 1)
    def _():
        total = parts[0][...].astype(jnp.float32)
        for part in parts[1:]:
            total = total + part[...].astype(jnp.float32)
        out[0] = (residual[...].astype(jnp.float32) + total).astype(jnp.bfloat16)

    @pl.when(section == sections - 2)
    def _():
        out[0] = third[...]

    @pl.when(section < sections - 2)
    def _():
        out[0, :, :width] = jnp.where(group == 0, first[...], second[...])
        out[0, :, width:] = jnp.where(group == 0, second[...], first[...])


def finish(parts, residual, third, earlier):
    return pl.pallas_call(
        functools.partial(finish_kernel, ways=len(parts)),
        out_shape=jax.ShapeDtypeStruct((1,) + residual.shape, jnp.bfloat16),
        in_specs=[VMEM] * (len(parts) + 4),
        out_specs=VMEM,
        name="finish",
        compiler_params=pltpu.CompilerParams(vmem_limit_bytes=4 << 20),
    )(*parts, residual, third, *earlier)


def stationary_body(token_ids, embed_columns, norm_gain, qkv_weight, out_weight):
    seq_count = lax.axis_size("seq")
    sections = lax.axis_size("section")
    ways = lax.axis_size("tp")
    s, c, t = lax.axis_index("seq"), lax.axis_index("section"), lax.axis_index("tp")
    block = token_ids.shape[0]
    rows = block * seq_count
    width = embed_columns.shape[0]
    half = qkv_weight.shape[1]
    features = half * seq_count
    heads = (QUERY_HEADS // ways, KEY_VALUE_HEADS // ways)

    def at(seq, section, tp):
        return (seq * sections + section) * ways + tp

    def moved(value, pairs):
        return lax.ppermute(value, AXES, pairs)

    gain = lax.dynamic_slice_in_dim(norm_gain, s * half, half, axis=1).astype(jnp.float32)
    cosine, sine = (jnp.asarray(table) for table in full_rope_tables(rows, HEAD_WIDTH))

    def partner(section):
        return section ^ 1

    everywhere = [(s1, t1) for s1 in range(seq_count) for t1 in range(ways)]

    lent = lax.ppermute(out_weight, "section", [(i, partner(i)) for i in range(sections)])
    end = sections - 1
    lent_far = moved(out_weight, [(at(s1, end, t1), at(1 - s1, partner(end), t1)) for s1, t1 in everywhere])

    other_ids = lax.ppermute(token_ids, "seq", [(0, 1), (1, 0)])
    servers = {0: lambda t1: 1, 1: lambda t1: 2 + t1 // 2}
    ids = jnp.where(c == 1, token_ids, other_ids)
    looked = lookup(ids, embed_columns)
    arrivals = {}
    for group in range(2):
        for k in send_order(ways):
            pairs = []
            for s1, t1 in everywhere:
                b = s1 * ways + (t1 - k) % ways
                pairs.append((at(b % seq_count, servers[group](t1), b // seq_count), at(s1, 0, t1)))
            arrivals[k, group] = moved(looked, pairs)
    staged = stage(qkv_weight, looked)
    pieces = [arrivals[k, group] for k in send_order(ways) for group in range(2)]

    def shifted(source, target, k):
        if k == 0 and partner(source) == target:
            return [(at(s1, i, t1), at(s1, partner(i), t1)) for i in range(source % 2, sections, 2) for s1, t1 in everywhere]
        return [(at(s1, source, t1), at(s1, target, (t1 + k) % ways)) for s1, t1 in everywhere]

    def crossed(source):
        return [
            (at(s1, i, t1), at(1 - s1, partner(i), t1))
            for i in (range(0, sections, 2) if source % 2 == 0 else [source])
            for s1, t1 in everywhere
        ]

    state = jnp.zeros((rows, width), jnp.bfloat16)
    earlier = []
    for layer in range(sections):
        aside = partner(layer)
        message, *kept = project(layer, pieces, gain, staged, ways, layer == end)
        if layer == end - 1:
            state, _ = lax.optimization_barrier((state, message))
            for m in range(2):
                chosen = lax.dynamic_slice_in_dim(state, lax.rem(t + m, 2) * block, block, axis=0)
                pairs = []
                for section in range(end - 1):
                    for s2, t2 in everywhere:
                        pairs.append((at(s2, section, t2), at((t2 + m) % 2, section, 2 * s2 + t2 // 2)))
                earlier.append(moved(chosen, pairs))
        got_far = moved(message, crossed(layer))
        got_near = moved(message, shifted(layer, aside, 0))
        if layer == end:
            break
        outs = attend(aside, got_far, got_near, cosine, sine, [lent], ways, block, features, heads)
        parts = [moved(outs[k], shifted(aside, layer, k)) for k in send_order(ways)]
        fresh = combine(parts, kept[0])
        if layer == end - 1:
            staged = stage(qkv_weight, fresh, end)
        else:
            state = jnp.where(c == layer, fresh, state)
        pieces = [moved(fresh, shifted(layer, layer + 1, k)) for k in send_order(ways)]

    mine, other = kept
    brought = moved(other, [(at(t1 // 2, end, t1), at(1 - t1 // 2, end, t1)) for t1 in range(ways)])
    residual = jnp.where(s == t // 2, mine, brought)
    outs = attend(aside, got_far, got_near, cosine, sine, [lent, lent_far], ways, block, features, heads)
    parts = [moved(outs[k], shifted(partner(end), end, k)) for k in send_order(ways)]
    third = moved(residual, shifted(end, partner(end), 0))
    return finish(parts, residual, third, earlier)


def passed_along(value, axis, steps):
    count = lax.axis_size(axis)
    leading, last = (max(0, -steps), min(count, count - steps))
    return lax.ppermute(value, axis, [(source, source + steps) for source in range(leading, last)])


def from_root(value, axis, root):
    mine = lax.axis_index(axis) == root
    return lax.psum(jnp.where(mine, value, jnp.zeros_like(value)), axis)


def rotate_half(heads, cosine_table, sine_values):
    half_width = heads.shape[-1] // 2
    first_half = heads[..., :half_width]
    second = heads[..., half_width:]
    cosine_table = cosine_table[:, None, :]
    sine_values = sine_values[:, None, :]
    return jnp.concatenate(
        [
            first_half * cosine_table - second * sine_values,
            second * cosine_table + first_half * sine_values,
        ],
        axis=-1,
    )


def norm_rows(row_block, gain_row):
    values = row_block.astype(jnp.float32)
    inverse_rms = lax.rsqrt(jnp.mean(values * values, axis=-1, keepdims=True) + EPS)
    return (values * inverse_rms * gain_row[None, :]).astype(jnp.bfloat16)


def gathered_project(full_rows, gain_row, qkv_full, positions, query_heads, key_value_heads):
    row_count = full_rows.shape[0]
    normed = norm_rows(full_rows, gain_row)
    projected_rows = jnp.dot(normed, qkv_full, preferred_element_type=jnp.float32)
    projected_rows = projected_rows.reshape(row_count, query_heads + 2 * key_value_heads, HEAD_WIDTH)
    cosine_table, sine_values = rope_tables(positions, HEAD_WIDTH)
    query_rows = rotate_half(projected_rows[:, :query_heads], cosine_table, sine_values)
    key_head_rows = rotate_half(
        projected_rows[:, query_heads : query_heads + key_value_heads], cosine_table, sine_values
    )
    value_head_rows = projected_rows[:, query_heads + key_value_heads :]
    return tuple(v.astype(jnp.bfloat16) for v in (query_rows, key_head_rows, value_head_rows))


def gathered_attend(query_rows, key_head_rows, value_head_rows, allowed):
    row_count, query_heads, head_size = query_rows.shape
    key_value_heads = key_head_rows.shape[1]
    query_groups = query_rows.reshape(row_count, key_value_heads, query_heads // key_value_heads, head_size)
    scores = jnp.einsum(
        "rkph,ckh->kprc", query_groups, key_head_rows, preferred_element_type=jnp.float32
    ) * head_size ** (-0.5)
    scores = jnp.where(allowed[None, None], scores, MASKED)
    weights = jax.nn.softmax(scores, axis=-1).astype(jnp.bfloat16)
    attended = jnp.einsum("kprc,ckh->rkph", weights, value_head_rows, preferred_element_type=jnp.float32)
    return attended.reshape(row_count, query_heads * head_size).astype(jnp.bfloat16)


def gathered_combine(current, attended, out_full):
    partial_value = lax.dot_general(
        attended, out_full, (((1,), (1,)), ((), ())), preferred_element_type=jnp.float32
    )
    summed = lax.psum_scatter(
        partial_value.astype(jnp.bfloat16), "tp", scatter_dimension=1, tiled=True
    ).astype(jnp.float32)
    return (current.astype(jnp.float32) + summed).astype(jnp.bfloat16)


def gathered_body(token_ids, embed_columns, norm_gain, qkv_weight, out_weight):
    seq_count = lax.axis_size("seq")
    section_count = lax.axis_size("section")
    tensor_parallel_count = lax.axis_size("tp")
    group_index = lax.axis_index("seq")
    section_index = lax.axis_index("section")
    block_row_slice = token_ids.shape[0]
    feature_cols = embed_columns.shape[0] * seq_count
    query_heads = QUERY_HEADS // tensor_parallel_count
    key_value_heads = KEY_VALUE_HEADS // tensor_parallel_count
    every_id = lax.all_gather(token_ids, "seq", axis=0, tiled=True)
    looked = jnp.take(embed_columns, every_id, axis=1)
    current = lax.all_to_all(looked, "seq", split_axis=1, concat_axis=0, tiled=True).T
    qkv_full = lax.all_gather(qkv_weight, "seq", axis=1, tiled=True)[0]
    out_full = lax.all_gather(out_weight, "seq", axis=1, tiled=True)[0]
    gain_row = norm_gain[0].astype(jnp.float32)
    outputs = jnp.zeros((block_row_slice, feature_cols), jnp.bfloat16)
    row_ids = jnp.arange(block_row_slice)[:, None]
    column = jnp.arange(2 * block_row_slice)[None, :]
    positions = group_index * block_row_slice + jnp.arange(block_row_slice)
    allowed = jnp.where(column < block_row_slice, group_index > 0, column - block_row_slice <= row_ids)
    for step_number in range(section_count):
        full_rows = lax.all_gather(current, "tp", axis=1, tiled=True)
        query_rows, key_head_rows, value_head_rows = gathered_project(
            full_rows, gain_row, qkv_full, positions, query_heads, key_value_heads
        )
        anchor_heads = from_root(key_head_rows, "seq", 0)
        anchor_values = from_root(value_head_rows, "seq", 0)
        both_keys = jnp.concatenate([anchor_heads, key_head_rows], axis=0)
        both_values = jnp.concatenate([anchor_values, value_head_rows], axis=0)
        attended = gathered_attend(query_rows, both_keys, both_values, allowed)
        new_rows = gathered_combine(current, attended, out_full)
        outputs = jnp.where(section_index == step_number, new_rows, outputs)
        if step_number + 1 < section_count:
            current = passed_along(new_rows, "section", 1)
    return outputs[None]


def solution(mesh):
    placed = (
        P("seq"),
        P(("tp", "seq"), None),
        P("section", None),
        P("section", "seq", "tp"),
        P("section", "seq", "tp"),
    )
    sizes = mesh.shape
    small = sizes["seq"] == 2 and sizes["tp"] == 4 and sizes["section"] == 4
    return jax.shard_map(
        stationary_body if small else gathered_body,
        mesh=mesh,
        in_specs=placed,
        out_specs=P("section", "seq", "tp"),
        check_vma=False,
    )
```

profile of v0, /device:TPU:11, one launch (start us, length us, event | category | flops | bytes accessed | tf_op | source)
XLA Modules:
  0.0 140.7 jit_solution(7924092007196506991)
XLA Ops:
  1.9 1.3 collective-permute-done
  3.2 7.7 %lookup.1.after = bf16[64,512]{1,0:T(8,128)(2,1)S(1)} custom-call(s32[64]{0:T(128)S(1)} %broadcast_select_fusion.1.ids_smem, s32[1,64]{1,0:T(1,128)S(1)} %bitcast.1, bf16[512,65536]{1,0:T(8,128)(2,1)} %table.1), custom_call_target="tpu_custom_call" | custom-call | tf_op jit(solution)/shard_map/lookup/pallas_call | solution.py:98
  16.4 6.2 %collective-permute-start.8 = (bf16[64,512]{1,0:T(8,128)(2,1)S(1)}, bf16[64,512]{1,0:T(8,128)(2,1)S(1)}, u32[]{:S(2)}, u32[]{:S(2)}) collective-permute-start(bf16[64,512]{1,0:T(8,128)(2,1)S(1)} %lookup.1.after), channel_id=1, source_target_pairs={{8,0},{24,1},{13,2},{29,3},{10,16},{26,17},{15,18},{31,19}} | collective-permute-start | bytes 196616 | tf_op jit(solution)/shard_map/ppermute | solution.py:388
  22.6 2.2 %copy-done = bf16[1,2048,1024]{2,1,0:T(8,128)(2,1)S(1)} copy-done((bf16[1,2048,1024]{2,1,0:T(8,128)(2,1)S(1)}, bf16[1,2048,1024]{2,1,0:T(8,128)(2,1)}, u32[]{:S(2)}) %copy-start) | copy-done | bytes 4194328
  27.8 7.1 %collective-permute-start.42 = (bf16[1,2048,512]{2,1,0:T(8,128)(2,1)}, bf16[1,2048,512]{2,1,0:T(8,128)(2,1)}, u32[]{:S(2)}, u32[]{:S(2)}) collective-permute-start(bf16[1,2048,512]{2,1,0:T(8,128)(2,1)} %param.11), channel_id=1, source_target_pairs={{12,24},{13,25},{14,26},{15,27},{28,8},{29,9},{30,10},{31,11}} | collective-permute-start | bytes 6291464 | tf_op jit(solution)/shard_map/ppermute | solution.py:388
  38.1 2.9 %collective-permute-start.15 = (bf16[128,512]{1,0:T(8,128)(2,1)S(1)}, bf16[128,512]{1,0:T(8,128)(2,1)S(1)}, u32[]{:S(2)}, u32[]{:S(2)}) collective-permute-start(bf16[128,512]{1,0:T(8,128)(2,1)S(1)} %get-tuple-element.35), channel_id=1, source_target_pairs={{4,0},{5,1},{6,2},{7,3},{20,16},{21,17},{22,18},{23,19},{12,8},{13... | collective-permute-start | bytes 393224 | tf_op jit(solution)/shard_map/ppermute | solution.py:388
  45.4 1.9 %collective-permute-done.19.refs_3_ = bf16[128,512]{1,0:T(8,128)(2,1)S(1)} collective-permute-done((bf16[128,512]{1,0:T(8,128)(2,1)S(1)}, bf16[128,512]{1,0:T(8,128)(2,1)S(1)}, u32[]{:S(2)}, u32[]{:S(2)}) %collective-permute-start.19) | collective-permute-done | bytes 131104 | tf_op jit(solution)/shard_map/ppermute | solution.py:388
  48.0 2.1 %collective-permute-start.21 = (bf16[128,1152]{1,0:T(8,128)(2,1)S(1)}, bf16[128,1152]{1,0:T(8,128)(2,1)S(1)}, u32[]{:S(2)}, u32[]{:S(2)}) collective-permute-start(bf16[128,1152]{1,0:T(8,128)(2,1)S(1)} %get-tuple-element.37), channel_id=1, source_target_pairs={{4,0},{5,1},{6,2},{7,3},{20,16},{21,17},{22,18},{23,19},{12,8},{13... | collective-permute-start | bytes 884744 | tf_op jit(solution)/shard_map/ppermute | solution.py:388
  54.6 1.9 %collective-permute-done.25.refs_3_ = bf16[128,512]{1,0:T(8,128)(2,1)S(1)} collective-permute-done((bf16[128,512]{1,0:T(8,128)(2,1)S(1)}, bf16[128,512]{1,0:T(8,128)(2,1)S(1)}, u32[]{:S(2)}, u32[]{:S(2)}) %collective-permute-start.25) | collective-permute-done | bytes 131104 | tf_op jit(solution)/shard_map/ppermute | solution.py:388
  62.0 33.8 %collective-permute-done.30.refs_0_ = bf16[128,1152]{1,0:T(8,128)(2,1)S(1)} collective-permute-done((bf16[128,1152]{1,0:T(8,128)(2,1)S(1)}, bf16[128,1152]{1,0:T(8,128)(2,1)S(1)}, u32[]{:S(2)}, u32[]{:S(2)}) %collective-permute-start.30) | collective-permute-done | bytes 294944 | tf_op jit(solution)/shard_map/ppermute | solution.py:388
  95.8 2.6 %attend.6 = (bf16[128,512]{1,0:T(8,128)(2,1)S(1)}, bf16[128,512]{1,0:T(8,128)(2,1)S(1)}, bf16[128,512]{1,0:T(8,128)(2,1)S(1)}, bf16[128,512]{1,0:T(8,128)(2,1)S(1)}) custom-call(bf16[128,1152]{1,0:T(8,128)(2,1)S(1)} %collective-permute-done.30.refs_0_, bf16[128,1152]{1,0:T(8,128)(2,1)S(1)} %collective-permute-done.31.refs_1_, f32[128,128]{1,0:T(8,128)S(1)} %copy-done.2, ...), custom_call_target="tpu_custom_call" | custom-call | tf_op jit(solution)/shard_map/attend/pallas_call | solution.py:298
  98.4 1.3 collective-permute-start.32
  99.7 1.3 collective-permute-start.33
  102.3 1.3 collective-permute-start.35
  104.4 2.1 %collective-permute-done.34.refs_2_ = bf16[128,512]{1,0:T(8,128)(2,1)S(1)} collective-permute-done((bf16[128,512]{1,0:T(8,128)(2,1)S(1)}, bf16[128,512]{1,0:T(8,128)(2,1)S(1)}, u32[]{:S(2)}, u32[]{:S(2)}) %collective-permute-start.34) | collective-permute-done | bytes 131104 | tf_op jit(solution)/shard_map/ppermute | solution.py:388
  110.5 1.5 %collective-permute-start.39 = (bf16[128,512]{1,0:T(8,128)(2,1)S(1)}, bf16[128,512]{1,0:T(8,128)(2,1)S(1)}, u32[]{:S(2)}, u32[]{:S(2)}) collective-permute-start(bf16[128,512]{1,0:T(8,128)(2,1)S(1)} %combine.5.after), channel_id=1, source_target_pairs={{0,4},{1,5},{2,6},{3,7},{16,20},{17,21},{18,22},{19,23},{8,12},{9,... | collective-permute-start | bytes 393224 | tf_op jit(solution)/shard_map/ppermute | solution.py:388
  112.1 2.2 %copy-done.1 = bf16[1,2048,1024]{2,1,0:T(8,128)(2,1)S(1)} copy-done((bf16[1,2048,1024]{2,1,0:T(8,128)(2,1)S(1)}, bf16[1,2048,1024]{2,1,0:T(8,128)(2,1)}, u32[]{:S(2)}) %copy-start.1) | copy-done | bytes 4194328
  114.6 2.6 %collective-permute-done.38.refs_2_ = bf16[128,512]{1,0:T(8,128)(2,1)S(1)} collective-permute-done((bf16[128,512]{1,0:T(8,128)(2,1)S(1)}, bf16[128,512]{1,0:T(8,128)(2,1)S(1)}, u32[]{:S(2)}, u32[]{:S(2)}) %collective-permute-start.38) | collective-permute-done | bytes 131104 | tf_op jit(solution)/shard_map/ppermute | solution.py:388
  118.1 2.3 %collective-permute-start.47 = (bf16[64,1024]{1,0:T(8,128)(2,1)S(1)}, bf16[64,1024]{1,0:T(8,128)(2,1)S(1)}, u32[]{:S(2)}, u32[]{:S(2)}) collective-permute-start(bf16[64,1024]{1,0:T(8,128)(2,1)S(1)} %get-tuple-element.55), channel_id=1, source_target_pairs={{12,28},{13,29},{30,14},{31,15}} | collective-permute-start | bytes 393224 | tf_op jit(solution)/shard_map/ppermute | solution.py:388
  120.4 1.3 collective-permute-start.40
  121.7 1.3 collective-permute-start.41
  124.5 1.3 collective-permute-start.48
  131.1 5.1 %collective-permute-done.43.refs_0_ = bf16[64,1024]{1,0:T(8,128)(2,1)S(1)} collective-permute-done((bf16[64,1024]{1,0:T(8,128)(2,1)S(1)}, bf16[64,1024]{1,0:T(8,128)(2,1)S(1)}, u32[]{:S(2)}, u32[]{:S(2)}) %collective-permute-start.43) | collective-permute-done | bytes 131104 | tf_op jit(solution)/shard_map/ppermute | solution.py:388
  136.2 3.7 %collective-permute-done.45.refs_2_ = bf16[64,1024]{1,0:T(8,128)(2,1)S(1)} collective-permute-done((bf16[64,1024]{1,0:T(8,128)(2,1)S(1)}, bf16[64,1024]{1,0:T(8,128)(2,1)S(1)}, u32[]{:S(2)}, u32[]{:S(2)}) %collective-permute-start.45) | collective-permute-done | bytes 131104 | tf_op jit(solution)/shard_map/ppermute | solution.py:388
  (108 shorter events, 42.7 us)
Async XLA Ops:
  0.0 36.0 %collective-permute-start.11 = (bf16[1,2048,512]{2,1,0:T(8,128)(2,1)}, bf16[1,2048,512]{2,1,0:T(8,128)(2,1)S(1)}, u32[]{:S(2)}, u32[]{:S(2)}) collective-permute-start(bf16[1,2048,512]{2,1,0:T(8,128)(2,1)} %param.11), channel_id=1, source_target_pairs={{0,4},{4,0},{8,12},{12,8},{1,5},{5,1},{9,13},{13,9},{2,6},{6,2},{1... | collective-permute-start | bytes 6291464 | tf_op jit(solution)/shard_map/ppermute | solution.py:398
  14.3 10.8 %collective-permute-start.5 = (bf16[64,512]{1,0:T(8,128)(2,1)S(1)}, bf16[64,512]{1,0:T(8,128)(2,1)S(1)}, u32[]{:S(2)}, u32[]{:S(2)}) collective-permute-start(bf16[64,512]{1,0:T(8,128)(2,1)S(1)} %lookup.1.after), channel_id=1, source_target_pairs={{20,0},{5,1},{21,2},{4,3},{22,16},{7,17},{23,18},{6,19}} | collective-permute-start | bytes 196616 | tf_op jit(solution)/shard_map/ppermute | solution.py:388
  15.0 10.2 %collective-permute-start.6 = (bf16[64,512]{1,0:T(8,128)(2,1)S(1)}, bf16[64,512]{1,0:T(8,128)(2,1)S(1)}, u32[]{:S(2)}, u32[]{:S(2)}) collective-permute-start(bf16[64,512]{1,0:T(8,128)(2,1)S(1)} %lookup.1.after), channel_id=1, source_target_pairs={{24,0},{9,1},{29,2},{12,3},{26,16},{11,17},{31,18},{14,19}} | collective-permute-start | bytes 196616 | tf_op jit(solution)/shard_map/ppermute | solution.py:388
  15.7 9.5 %collective-permute-start.7 = (bf16[64,512]{1,0:T(8,128)(2,1)S(1)}, bf16[64,512]{1,0:T(8,128)(2,1)S(1)}, u32[]{:S(2)}, u32[]{:S(2)}) collective-permute-start(bf16[64,512]{1,0:T(8,128)(2,1)S(1)} %lookup.1.after), channel_id=1, source_target_pairs={{4,0},{20,1},{5,2},{21,3},{6,16},{22,17},{7,18},{23,19}} | collective-permute-start | bytes 196616 | tf_op jit(solution)/shard_map/ppermute | solution.py:388
  16.4 8.8 %collective-permute-start.8 = (bf16[64,512]{1,0:T(8,128)(2,1)S(1)}, bf16[64,512]{1,0:T(8,128)(2,1)S(1)}, u32[]{:S(2)}, u32[]{:S(2)}) collective-permute-start(bf16[64,512]{1,0:T(8,128)(2,1)S(1)} %lookup.1.after), channel_id=1, source_target_pairs={{8,0},{24,1},{13,2},{29,3},{10,16},{26,17},{15,18},{31,19}} | collective-permute-start | bytes 196616 | tf_op jit(solution)/shard_map/ppermute | solution.py:388
  25.2 9.7 %collective-permute-start.10 = (bf16[128,1152]{1,0:T(8,128)(2,1)S(1)}, bf16[128,1152]{1,0:T(8,128)(2,1)S(1)}, u32[]{:S(2)}, u32[]{:S(2)}) collective-permute-start(bf16[128,1152]{1,0:T(8,128)(2,1)S(1)} %get-tuple-element.31), channel_id=1, source_target_pairs={{0,4},{1,5},{2,6},{3,7},{16,20},{17,21},{18,22},{19,23},{8,12},{9,... | collective-permute-start | bytes 884744 | tf_op jit(solution)/shard_map/ppermute | solution.py:388
  26.5 9.5 %collective-permute-start.9 = (bf16[128,1152]{1,0:T(8,128)(2,1)S(1)}, bf16[128,1152]{1,0:T(8,128)(2,1)S(1)}, u32[]{:S(2)}, u32[]{:S(2)}) collective-permute-start(bf16[128,1152]{1,0:T(8,128)(2,1)S(1)} %get-tuple-element.31), channel_id=1, source_target_pairs={{0,20},{1,21},{2,22},{3,23},{16,4},{17,5},{18,6},{19,7},{8,28},{9,... | collective-permute-start | bytes 884744 | tf_op jit(solution)/shard_map/ppermute | solution.py:388
  27.8 96.6 %collective-permute-start.42 = (bf16[1,2048,512]{2,1,0:T(8,128)(2,1)}, bf16[1,2048,512]{2,1,0:T(8,128)(2,1)}, u32[]{:S(2)}, u32[]{:S(2)}) collective-permute-start(bf16[1,2048,512]{2,1,0:T(8,128)(2,1)} %param.11), channel_id=1, source_target_pairs={{12,24},{13,25},{14,26},{15,27},{28,8},{29,9},{30,10},{31,11}} | collective-permute-start | bytes 6291464 | tf_op jit(solution)/shard_map/ppermute | solution.py:388
  59.4 36.4 %collective-permute-start.30 = (bf16[128,1152]{1,0:T(8,128)(2,1)S(1)}, bf16[128,1152]{1,0:T(8,128)(2,1)S(1)}, u32[]{:S(2)}, u32[]{:S(2)}) collective-permute-start(bf16[128,1152]{1,0:T(8,128)(2,1)S(1)} %get-tuple-element.43), channel_id=1, source_target_pairs={{0,20},{1,21},{2,22},{3,23},{16,4},{17,5},{18,6},{19,7},{8,28},{9,... | collective-permute-start | bytes 884744 | tf_op jit(solution)/shard_map/ppermute | solution.py:388
  60.7 35.1 %collective-permute-start.31 = (bf16[128,1152]{1,0:T(8,128)(2,1)S(1)}, bf16[128,1152]{1,0:T(8,128)(2,1)S(1)}, u32[]{:S(2)}, u32[]{:S(2)}) collective-permute-start(bf16[128,1152]{1,0:T(8,128)(2,1)S(1)} %get-tuple-element.43), channel_id=1, source_target_pairs={{0,4},{1,5},{2,6},{3,7},{16,20},{17,21},{18,22},{19,23},{8,12},{9,... | collective-permute-start | bytes 884744 | tf_op jit(solution)/shard_map/ppermute | solution.py:388
  101.0 5.5 %collective-permute-start.34 = (bf16[128,512]{1,0:T(8,128)(2,1)S(1)}, bf16[128,512]{1,0:T(8,128)(2,1)S(1)}, u32[]{:S(2)}, u32[]{:S(2)}) collective-permute-start(bf16[128,512]{1,0:T(8,128)(2,1)S(1)} %get-tuple-element.46), channel_id=1, source_target_pairs={{12,11},{13,8},{14,9},{15,10},{28,27},{29,24},{30,25},{31,26}} | collective-permute-start | bytes 393224 | tf_op jit(solution)/shard_map/ppermute | solution.py:388
  106.6 7.9 %collective-permute-start.36 = (bf16[128,512]{1,0:T(8,128)(2,1)S(1)}, bf16[128,512]{1,0:T(8,128)(2,1)S(1)}, u32[]{:S(2)}, u32[]{:S(2)}) collective-permute-start(bf16[128,512]{1,0:T(8,128)(2,1)S(1)} %combine.5.after), channel_id=1, source_target_pairs={{8,14},{9,15},{10,12},{11,13},{24,30},{25,31},{26,28},{27,29}} | collective-permute-start | bytes 393224 | tf_op jit(solution)/shard_map/ppermute | solution.py:388
  107.9 6.7 %collective-permute-start.37 = (bf16[128,512]{1,0:T(8,128)(2,1)S(1)}, bf16[128,512]{1,0:T(8,128)(2,1)S(1)}, u32[]{:S(2)}, u32[]{:S(2)}) collective-permute-start(bf16[128,512]{1,0:T(8,128)(2,1)S(1)} %combine.5.after), channel_id=1, source_target_pairs={{8,13},{9,14},{10,15},{11,12},{24,29},{25,30},{26,31},{27,28}} | collective-permute-start | bytes 393224 | tf_op jit(solution)/shard_map/ppermute | solution.py:388
  109.2 8.0 %collective-permute-start.38 = (bf16[128,512]{1,0:T(8,128)(2,1)S(1)}, bf16[128,512]{1,0:T(8,128)(2,1)S(1)}, u32[]{:S(2)}, u32[]{:S(2)}) collective-permute-start(bf16[128,512]{1,0:T(8,128)(2,1)S(1)} %combine.5.after), channel_id=1, source_target_pairs={{8,15},{9,12},{10,13},{11,14},{24,31},{25,28},{26,29},{27,30}} | collective-permute-start | bytes 393224 | tf_op jit(solution)/shard_map/ppermute | solution.py:388
  110.5 6.8 %collective-permute-start.39 = (bf16[128,512]{1,0:T(8,128)(2,1)S(1)}, bf16[128,512]{1,0:T(8,128)(2,1)S(1)}, u32[]{:S(2)}, u32[]{:S(2)}) collective-permute-start(bf16[128,512]{1,0:T(8,128)(2,1)S(1)} %combine.5.after), channel_id=1, source_target_pairs={{0,4},{1,5},{2,6},{3,7},{16,20},{17,21},{18,22},{19,23},{8,12},{9,... | collective-permute-start | bytes 393224 | tf_op jit(solution)/shard_map/ppermute | solution.py:388
  118.1 5.6 %collective-permute-start.47 = (bf16[64,1024]{1,0:T(8,128)(2,1)S(1)}, bf16[64,1024]{1,0:T(8,128)(2,1)S(1)}, u32[]{:S(2)}, u32[]{:S(2)}) collective-permute-start(bf16[64,1024]{1,0:T(8,128)(2,1)S(1)} %get-tuple-element.55), channel_id=1, source_target_pairs={{12,28},{13,29},{30,14},{31,15}} | collective-permute-start | bytes 393224 | tf_op jit(solution)/shard_map/ppermute | solution.py:388
  120.4 5.4 %collective-permute-start.40 = (bf16[128,1152]{1,0:T(8,128)(2,1)S(1)}, bf16[128,1152]{1,0:T(8,128)(2,1)S(1)}, u32[]{:S(2)}, u32[]{:S(2)}) collective-permute-start(bf16[128,1152]{1,0:T(8,128)(2,1)S(1)} %get-tuple-element.49), channel_id=1, source_target_pairs={{12,24},{13,25},{14,26},{15,27},{28,8},{29,9},{30,10},{31,11}} | collective-permute-start | bytes 884744 | tf_op jit(solution)/shard_map/ppermute | solution.py:388
  123.1 5.4 %collective-permute-start.49 = (bf16[64,512]{1,0:T(8,128)(2,1)S(1)}, bf16[64,512]{1,0:T(8,128)(2,1)S(1)}, u32[]{:S(2)}, u32[]{:S(2)}) collective-permute-start(bf16[64,512]{1,0:T(8,128)(2,1)S(1)} %get-tuple-element.58), channel_id=1, source_target_pairs={{0,0},{1,16},{2,1},{3,17},{16,2},{17,18},{18,3},{19,19},{4,4},{5,2... | collective-permute-start | bytes 196616 | tf_op jit(solution)/shard_map/ppermute | solution.py:388
  123.8 6.0 %collective-permute-start.50 = (bf16[64,512]{1,0:T(8,128)(2,1)S(1)}, bf16[64,512]{1,0:T(8,128)(2,1)S(1)}, u32[]{:S(2)}, u32[]{:S(2)}) collective-permute-start(bf16[64,512]{1,0:T(8,128)(2,1)S(1)} %get-tuple-element.57), channel_id=1, source_target_pairs={{0,16},{1,0},{2,17},{3,1},{16,18},{17,2},{18,19},{19,3},{4,20},{5,... | collective-permute-start | bytes 196616 | tf_op jit(solution)/shard_map/ppermute | solution.py:388
  124.5 6.6 %collective-permute-start.48 = (bf16[64,1024]{1,0:T(8,128)(2,1)S(1)}, bf16[64,1024]{1,0:T(8,128)(2,1)S(1)}, u32[]{:S(2)}, u32[]{:S(2)}) collective-permute-start(bf16[64,1024]{1,0:T(8,128)(2,1)S(1)} %broadcast_select_fusion.refs_4_), channel_id=1, source_target_pairs={{4,0},{5,1},{6,2},{7,3},{20,16},{21,17},{22,18},{23,19},{12,8},{13... | collective-permute-start | bytes 393224 | tf_op jit(solution)/shard_map/ppermute | solution.py:388
  125.8 10.4 %collective-permute-start.43 = (bf16[64,1024]{1,0:T(8,128)(2,1)S(1)}, bf16[64,1024]{1,0:T(8,128)(2,1)S(1)}, u32[]{:S(2)}, u32[]{:S(2)}) collective-permute-start(bf16[64,1024]{1,0:T(8,128)(2,1)S(1)} %get-tuple-element.50), channel_id=1, source_target_pairs={{8,14},{9,15},{10,12},{11,13},{24,30},{25,31},{26,28},{27,29}} | collective-permute-start | bytes 393224 | tf_op jit(solution)/shard_map/ppermute | solution.py:388
  127.1 9.1 %collective-permute-start.44 = (bf16[64,1024]{1,0:T(8,128)(2,1)S(1)}, bf16[64,1024]{1,0:T(8,128)(2,1)S(1)}, u32[]{:S(2)}, u32[]{:S(2)}) collective-permute-start(bf16[64,1024]{1,0:T(8,128)(2,1)S(1)} %get-tuple-element.51), channel_id=1, source_target_pairs={{8,13},{9,14},{10,15},{11,12},{24,29},{25,30},{26,31},{27,28}} | collective-permute-start | bytes 393224 | tf_op jit(solution)/shard_map/ppermute | solution.py:388
  128.4 11.5 %collective-permute-start.45 = (bf16[64,1024]{1,0:T(8,128)(2,1)S(1)}, bf16[64,1024]{1,0:T(8,128)(2,1)S(1)}, u32[]{:S(2)}, u32[]{:S(2)}) collective-permute-start(bf16[64,1024]{1,0:T(8,128)(2,1)S(1)} %get-tuple-element.52), channel_id=1, source_target_pairs={{8,15},{9,12},{10,13},{11,14},{24,31},{25,28},{26,29},{27,30}} | collective-permute-start | bytes 393224 | tf_op jit(solution)/shard_map/ppermute | solution.py:388
  129.8 10.2 %collective-permute-start.46 = (bf16[64,1024]{1,0:T(8,128)(2,1)S(1)}, bf16[64,1024]{1,0:T(8,128)(2,1)S(1)}, u32[]{:S(2)}, u32[]{:S(2)}) collective-permute-start(bf16[64,1024]{1,0:T(8,128)(2,1)S(1)} %get-tuple-element.53), channel_id=1, source_target_pairs={{0,4},{1,5},{2,6},{3,7},{16,20},{17,21},{18,22},{19,23},{8,12},{9,... | collective-permute-start | bytes 393224 | tf_op jit(solution)/shard_map/ppermute | solution.py:388
  (32 other events, 131.7 us)
where the time goes:
time: 142 us; the launch traced here: 141 us
  starting transfers between devices  65.8 us (46%)
  waiting for transfers between devices  56.7 us (40%)
  Pallas kernels  12.8 us (9%)
  local copies, waits for them, and re-layouts  4.4 us (3%)
    ppermute x49, starting transfers between devices, moved(): return lax.ppermute(value, AXES, pairs)  63.9 us
    ppermute x49, waiting for transfers between devices, moved(): return lax.ppermute(value, AXES, pairs)  55.4 us
    pallas_call x1, Pallas kernels, lookup(): pl.pallas_call(lookup_kernel, out_shape=jax.ShapeDtypeStruct((count, feat...  7.73 us
    unnamed x10, local copies, waits for them, and re-layouts  4.38 us
  transfers between devices with their start and end apart: 51, of which 13 were waited for; matrix products, arithmetic and copies ran while one was open for 0% of the time, Pallas kernels for 9%

commit v1 on v0

--- a/solution.py
+++ b/solution.py
@@ -174,23 +174,17 @@
     )(*pieces, gain, weight)
 
 
-def stage_kernel(weight, after, out, sem, *, section):
-    def bring():
-        copy = pltpu.make_async_copy(weight, out, sem)
-        copy.start()
-        copy.wait()
-
-    if section is None:
-        bring()
-    else:
-        pl.when(lax.axis_index("section") == section)(bring)
-
-
-def stage(weight, after, section=None):
+def stage_kernel(weight, after, out, sem):
+    copy = pltpu.make_async_copy(weight, out, sem)
+    copy.start()
+    copy.wait()
+
+
+def stage(section, weight, after):
     return pl.pallas_call(
-        functools.partial(stage_kernel, section=section),
+        on_section(stage_kernel, section),
         out_shape=jax.ShapeDtypeStruct(weight.shape, weight.dtype),
-        in_specs=[ANY if section is None else HBM, ANY],
+        in_specs=[HBM, ANY],
         out_specs=VMEM,
         scratch_shapes=[pltpu.SemaphoreType.DMA],
         name="stage",
@@ -227,18 +221,17 @@
     allowed = ((row_block == col_block) & (col <= row)) | ((col_block == 0) & (row_block > 0))
     keys = [rotated(query_heads + j) for j in range(key_value_heads)]
     held = [head(query_heads + key_value_heads + j).astype(jnp.bfloat16) for j in range(key_value_heads)]
-    results = []
-    for i in range(query_heads):
-        scores = lax.dot_general(
-            rotated(i, chosen), keys[i // repeat], (((1,), (1,)), ((), ())), preferred_element_type=jnp.float32
-        ) * HEAD_WIDTH ** (-0.5)
-        scores = jnp.where(allowed, scores, MASKED)
-        top = jnp.max(scores, axis=1, keepdims=True)
-        powers = jnp.exp(scores - top)
-        weights = (powers / jnp.sum(powers, axis=1, keepdims=True)).astype(jnp.bfloat16)
-        results.append(
-            jnp.dot(weights, held[i // repeat], preferred_element_type=jnp.float32).astype(jnp.bfloat16)
-        )
+    queries = [rotated(i, chosen) for i in range(query_heads)]
+    scores = [times_transposed(query, keys[i // repeat]) * HEAD_WIDTH ** (-0.5) for i, query in enumerate(queries)]
+    scores = [jnp.where(allowed, score, MASKED) for score in scores]
+    tops = [jnp.max(score, axis=1, keepdims=True) for score in scores]
+    powers = [jnp.exp(score - top) for score, top in zip(scores, tops)]
+    sums = [jnp.sum(power, axis=1, keepdims=True) for power in powers]
+    weights = [(power / total_power).astype(jnp.bfloat16) for power, total_power in zip(powers, sums)]
+    results = [
+        jnp.dot(weight, held[i // repeat], preferred_element_type=jnp.float32).astype(jnp.bfloat16)
+        for i, weight in enumerate(weights)
+    ]
     return jnp.concatenate(results, axis=1)
 
 
@@ -411,7 +404,7 @@
                 b = s1 * ways + (t1 - k) % ways
                 pairs.append((at(b % seq_count, servers[group](t1), b // seq_count), at(s1, 0, t1)))
             arrivals[k, group] = moved(looked, pairs)
-    staged = stage(qkv_weight, looked)
+    staged = stage(0, qkv_weight, looked)
     pieces = [arrivals[k, group] for k in send_order(ways) for group in range(2)]
 
     def shifted(source, target, k):
@@ -447,9 +440,8 @@
         outs = attend(aside, got_far, got_near, cosine, sine, [lent], ways, block, features, heads)
         parts = [moved(outs[k], shifted(aside, layer, k)) for k in send_order(ways)]
         fresh = combine(parts, kept[0])
-        if layer == end - 1:
-            staged = stage(qkv_weight, fresh, end)
-        else:
+        staged = stage(layer + 1, qkv_weight, fresh)
+        if layer < end - 1:
             state = jnp.where(c == layer, fresh, state)
         pieces = [moved(fresh, shifted(layer, layer + 1, k)) for k in send_order(ways)]
 
@@ -457,7 +449,9 @@
     brought = moved(other, [(at(t1 // 2, end, t1), at(1 - t1 // 2, end, t1)) for t1 in range(ways)])
     residual = jnp.where(s == t // 2, mine, brought)
     outs = attend(aside, got_far, got_near, cosine, sine, [lent, lent_far], ways, block, features, heads)
-    parts = [moved(outs[k], shifted(partner(end), end, k)) for k in send_order(ways)]
+    parts = []
+    for k in send_order(ways):
+        parts.append(moved(outs[k], shifted(partner(end), end, k)))
     third = moved(residual, shifted(end, partner(end), 0))
     return finish(parts, residual, third, earlier)
 

time: 142 us -> 138 us (0.972)
  waiting for transfers between devices: 56.7 us -> 53.7 us
    ppermute x49, waiting for transfers between devices: 55.4 us -> 52.4 us  [moved(): return lax.ppermute(value, AXES, pairs)]
    unnamed x10 -> x12, local copies, waits for them, and re-layouts: 4.38 us -> 4.39 us
  transfers between devices with their start and end apart: 51 -> 51, of which waited for: 13 -> 13; matrix products, arithmetic and copies ran while one was open for 0% -> 0% of each run, Pallas kernels for 9% -> 8%
where the time goes in v1:
time: 138 us; the launch traced here: 137 us
  starting transfers between devices  66.2 us (48%)
  waiting for transfers between devices  53.7 us (39%)
  Pallas kernels  11.7 us (8%)
  local copies, waits for them, and re-layouts  4.41 us (3%)
    ppermute x49, starting transfers between devices, moved(): return lax.ppermute(value, AXES, pairs)  64.3 us
    ppermute x49, waiting for transfers between devices, moved(): return lax.ppermute(value, AXES, pairs)  52.4 us
    pallas_call x1, Pallas kernels, lookup(): pl.pallas_call(lookup_kernel, out_shape=jax.ShapeDtypeStruct((count, feat...  7.73 us
    unnamed x12, local copies, waits for them, and re-layouts  4.39 us
  transfers between devices with their start and end apart: 51, of which 13 were waited for; matrix products, arithmetic and copies ran while one was open for 0% of the time, Pallas kernels for 8%

profile of v1, /device:TPU:11, one launch (start us, length us, event | category | flops | bytes accessed | tf_op | source)
XLA Modules:
  0.0 136.9 jit_solution(1247503447144177105)
XLA Ops:
  1.9 1.3 collective-permute-done
  3.2 7.7 %lookup.1.refs_1_ = bf16[64,512]{1,0:T(8,128)(2,1)S(1)} custom-call(s32[64]{0:T(128)S(1)} %broadcast_select_fusion.1.ids_smem, s32[1,64]{1,0:T(1,128)S(1)} %bitcast.1, bf16[512,65536]{1,0:T(8,128)(2,1)} %table.1), custom_call_target="tpu_custom_call" | custom-call | tf_op jit(solution)/shard_map/lookup/pallas_call | solution.py:98
  16.4 6.2 %collective-permute-start.8 = (bf16[64,512]{1,0:T(8,128)(2,1)S(1)}, bf16[64,512]{1,0:T(8,128)(2,1)S(1)}, u32[]{:S(2)}, u32[]{:S(2)}) collective-permute-start(bf16[64,512]{1,0:T(8,128)(2,1)S(1)} %lookup.1.refs_1_), channel_id=1, source_target_pairs={{8,0},{24,1},{13,2},{29,3},{10,16},{26,17},{15,18},{31,19}} | collective-permute-start | bytes 196616 | tf_op jit(solution)/shard_map/ppermute | solution.py:381
  22.6 2.2 %copy-done = bf16[1,2048,1024]{2,1,0:T(8,128)(2,1)S(1)} copy-done((bf16[1,2048,1024]{2,1,0:T(8,128)(2,1)S(1)}, bf16[1,2048,1024]{2,1,0:T(8,128)(2,1)}, u32[]{:S(2)}) %copy-start) | copy-done | bytes 4194328
  24.9 1.6 %collective-permute-start.10 = (bf16[128,1152]{1,0:T(8,128)(2,1)S(1)}, bf16[128,1152]{1,0:T(8,128)(2,1)S(1)}, u32[]{:S(2)}, u32[]{:S(2)}) collective-permute-start(bf16[128,1152]{1,0:T(8,128)(2,1)S(1)} %get-tuple-element.31), channel_id=1, source_target_pairs={{0,4},{1,5},{2,6},{3,7},{16,20},{17,21},{18,22},{19,23},{8,12},{9,... | collective-permute-start | bytes 884744 | tf_op jit(solution)/shard_map/ppermute | solution.py:381
  27.8 7.1 %collective-permute-start.42 = (bf16[1,2048,512]{2,1,0:T(8,128)(2,1)}, bf16[1,2048,512]{2,1,0:T(8,128)(2,1)}, u32[]{:S(2)}, u32[]{:S(2)}) collective-permute-start(bf16[1,2048,512]{2,1,0:T(8,128)(2,1)} %param.11), channel_id=1, source_target_pairs={{12,24},{13,25},{14,26},{15,27},{28,8},{29,9},{30,10},{31,11}} | collective-permute-start | bytes 6291464 | tf_op jit(solution)/shard_map/ppermute | solution.py:381
  38.1 2.9 %collective-permute-start.15 = (bf16[128,512]{1,0:T(8,128)(2,1)S(1)}, bf16[128,512]{1,0:T(8,128)(2,1)S(1)}, u32[]{:S(2)}, u32[]{:S(2)}) collective-permute-start(bf16[128,512]{1,0:T(8,128)(2,1)S(1)} %get-tuple-element.35), channel_id=1, source_target_pairs={{4,0},{5,1},{6,2},{7,3},{20,16},{21,17},{22,18},{23,19},{12,8},{13... | collective-permute-start | bytes 393224 | tf_op jit(solution)/shard_map/ppermute | solution.py:381
  45.4 1.9 %collective-permute-done.19.refs_3_ = bf16[128,512]{1,0:T(8,128)(2,1)S(1)} collective-permute-done((bf16[128,512]{1,0:T(8,128)(2,1)S(1)}, bf16[128,512]{1,0:T(8,128)(2,1)S(1)}, u32[]{:S(2)}, u32[]{:S(2)}) %collective-permute-start.19) | collective-permute-done | bytes 131104 | tf_op jit(solution)/shard_map/ppermute | solution.py:381
  48.0 2.1 %collective-permute-start.21 = (bf16[128,1152]{1,0:T(8,128)(2,1)S(1)}, bf16[128,1152]{1,0:T(8,128)(2,1)S(1)}, u32[]{:S(2)}, u32[]{:S(2)}) collective-permute-start(bf16[128,1152]{1,0:T(8,128)(2,1)S(1)} %get-tuple-element.37), channel_id=1, source_target_pairs={{4,0},{5,1},{6,2},{7,3},{20,16},{21,17},{22,18},{23,19},{12,8},{13... | collective-permute-start | bytes 884744 | tf_op jit(solution)/shard_map/ppermute | solution.py:381
  54.6 1.9 %collective-permute-done.25.refs_3_ = bf16[128,512]{1,0:T(8,128)(2,1)S(1)} collective-permute-done((bf16[128,512]{1,0:T(8,128)(2,1)S(1)}, bf16[128,512]{1,0:T(8,128)(2,1)S(1)}, u32[]{:S(2)}, u32[]{:S(2)}) %collective-permute-start.25) | collective-permute-done | bytes 131104 | tf_op jit(solution)/shard_map/ppermute | solution.py:381
  62.0 31.9 %collective-permute-done.30.refs_0_ = bf16[128,1152]{1,0:T(8,128)(2,1)S(1)} collective-permute-done((bf16[128,1152]{1,0:T(8,128)(2,1)S(1)}, bf16[128,1152]{1,0:T(8,128)(2,1)S(1)}, u32[]{:S(2)}, u32[]{:S(2)}) %collective-permute-start.30) | collective-permute-done | bytes 294944 | tf_op jit(solution)/shard_map/ppermute | solution.py:381
  94.0 1.7 %attend.6 = (bf16[128,512]{1,0:T(8,128)(2,1)S(1)}, bf16[128,512]{1,0:T(8,128)(2,1)S(1)}, bf16[128,512]{1,0:T(8,128)(2,1)S(1)}, bf16[128,512]{1,0:T(8,128)(2,1)S(1)}) custom-call(bf16[128,1152]{1,0:T(8,128)(2,1)S(1)} %collective-permute-done.30.refs_0_, bf16[128,1152]{1,0:T(8,128)(2,1)S(1)} %collective-permute-done.31.refs_1_, f32[128,128]{1,0:T(8,128)S(1)} %copy-done.3, ...), custom_call_target="tpu_custom_call" | custom-call | tf_op jit(solution)/shard_map/attend/pallas_call | solution.py:291
  95.7 1.3 collective-permute-start.32
  98.3 1.4 %collective-permute-start.34 = (bf16[128,512]{1,0:T(8,128)(2,1)S(1)}, bf16[128,512]{1,0:T(8,128)(2,1)S(1)}, u32[]{:S(2)}, u32[]{:S(2)}) collective-permute-start(bf16[128,512]{1,0:T(8,128)(2,1)S(1)} %get-tuple-element.46), channel_id=1, source_target_pairs={{12,11},{13,8},{14,9},{15,10},{28,27},{29,24},{30,25},{31,26}} | collective-permute-start | bytes 393224 | tf_op jit(solution)/shard_map/ppermute | solution.py:381
  99.7 1.3 collective-permute-start.35
  101.7 2.4 %collective-permute-done.34.refs_2_ = bf16[128,512]{1,0:T(8,128)(2,1)S(1)} collective-permute-done((bf16[128,512]{1,0:T(8,128)(2,1)S(1)}, bf16[128,512]{1,0:T(8,128)(2,1)S(1)}, u32[]{:S(2)}, u32[]{:S(2)}) %collective-permute-start.34) | collective-permute-done | bytes 131104 | tf_op jit(solution)/shard_map/ppermute | solution.py:381
  109.4 2.2 %copy-done.2 = bf16[1,2048,1024]{2,1,0:T(8,128)(2,1)S(1)} copy-done((bf16[1,2048,1024]{2,1,0:T(8,128)(2,1)S(1)}, bf16[1,2048,1024]{2,1,0:T(8,128)(2,1)}, u32[]{:S(2)}) %copy-start.2) | copy-done | bytes 4194328
  112.0 2.6 %collective-permute-done.38.refs_2_ = bf16[128,512]{1,0:T(8,128)(2,1)S(1)} collective-permute-done((bf16[128,512]{1,0:T(8,128)(2,1)S(1)}, bf16[128,512]{1,0:T(8,128)(2,1)S(1)}, u32[]{:S(2)}, u32[]{:S(2)}) %collective-permute-start.38) | collective-permute-done | bytes 131104 | tf_op jit(solution)/shard_map/ppermute | solution.py:381
  115.4 2.4 %collective-permute-start.47 = (bf16[64,1024]{1,0:T(8,128)(2,1)S(1)}, bf16[64,1024]{1,0:T(8,128)(2,1)S(1)}, u32[]{:S(2)}, u32[]{:S(2)}) collective-permute-start(bf16[64,1024]{1,0:T(8,128)(2,1)S(1)} %get-tuple-element.55), channel_id=1, source_target_pairs={{12,28},{13,29},{30,14},{31,15}} | collective-permute-start | bytes 393224 | tf_op jit(solution)/shard_map/ppermute | solution.py:381
  117.8 1.3 collective-permute-start.40
  119.1 1.3 collective-permute-start.41
  121.9 1.3 collective-permute-start.48
  128.5 4.0 %collective-permute-done.43.refs_0_ = bf16[64,1024]{1,0:T(8,128)(2,1)S(1)} collective-permute-done((bf16[64,1024]{1,0:T(8,128)(2,1)S(1)}, bf16[64,1024]{1,0:T(8,128)(2,1)S(1)}, u32[]{:S(2)}, u32[]{:S(2)}) %collective-permute-start.43) | collective-permute-done | bytes 131104 | tf_op jit(solution)/shard_map/ppermute | solution.py:381
  132.4 3.7 %collective-permute-done.45.refs_2_ = bf16[64,1024]{1,0:T(8,128)(2,1)S(1)} collective-permute-done((bf16[64,1024]{1,0:T(8,128)(2,1)S(1)}, bf16[64,1024]{1,0:T(8,128)(2,1)S(1)}, u32[]{:S(2)}, u32[]{:S(2)}) %collective-permute-start.45) | collective-permute-done | bytes 131104 | tf_op jit(solution)/shard_map/ppermute | solution.py:381
  (112 shorter events, 42.4 us)
Async XLA Ops:
  0.0 36.0 %collective-permute-start.11 = (bf16[1,2048,512]{2,1,0:T(8,128)(2,1)}, bf16[1,2048,512]{2,1,0:T(8,128)(2,1)S(1)}, u32[]{:S(2)}, u32[]{:S(2)}) collective-permute-start(bf16[1,2048,512]{2,1,0:T(8,128)(2,1)} %param.11), channel_id=1, source_target_pairs={{0,4},{4,0},{8,12},{12,8},{1,5},{5,1},{9,13},{13,9},{2,6},{6,2},{1... | collective-permute-start | bytes 6291464 | tf_op jit(solution)/shard_map/ppermute | solution.py:391
  14.3 10.6 %collective-permute-start.5 = (bf16[64,512]{1,0:T(8,128)(2,1)S(1)}, bf16[64,512]{1,0:T(8,128)(2,1)S(1)}, u32[]{:S(2)}, u32[]{:S(2)}) collective-permute-start(bf16[64,512]{1,0:T(8,128)(2,1)S(1)} %lookup.1.refs_1_), channel_id=1, source_target_pairs={{20,0},{5,1},{21,2},{4,3},{22,16},{7,17},{23,18},{6,19}} | collective-permute-start | bytes 196616 | tf_op jit(solution)/shard_map/ppermute | solution.py:381
  15.0 9.9 %collective-permute-start.6 = (bf16[64,512]{1,0:T(8,128)(2,1)S(1)}, bf16[64,512]{1,0:T(8,128)(2,1)S(1)}, u32[]{:S(2)}, u32[]{:S(2)}) collective-permute-start(bf16[64,512]{1,0:T(8,128)(2,1)S(1)} %lookup.1.refs_1_), channel_id=1, source_target_pairs={{24,0},{9,1},{29,2},{12,3},{26,16},{11,17},{31,18},{14,19}} | collective-permute-start | bytes 196616 | tf_op jit(solution)/shard_map/ppermute | solution.py:381
  15.7 9.2 %collective-permute-start.7 = (bf16[64,512]{1,0:T(8,128)(2,1)S(1)}, bf16[64,512]{1,0:T(8,128)(2,1)S(1)}, u32[]{:S(2)}, u32[]{:S(2)}) collective-permute-start(bf16[64,512]{1,0:T(8,128)(2,1)S(1)} %lookup.1.refs_1_), channel_id=1, source_target_pairs={{4,0},{20,1},{5,2},{21,3},{6,16},{22,17},{7,18},{23,19}} | collective-permute-start | bytes 196616 | tf_op jit(solution)/shard_map/ppermute | solution.py:381
  16.4 8.5 %collective-permute-start.8 = (bf16[64,512]{1,0:T(8,128)(2,1)S(1)}, bf16[64,512]{1,0:T(8,128)(2,1)S(1)}, u32[]{:S(2)}, u32[]{:S(2)}) collective-permute-start(bf16[64,512]{1,0:T(8,128)(2,1)S(1)} %lookup.1.refs_1_), channel_id=1, source_target_pairs={{8,0},{24,1},{13,2},{29,3},{10,16},{26,17},{15,18},{31,19}} | collective-permute-start | bytes 196616 | tf_op jit(solution)/shard_map/ppermute | solution.py:381
  24.9 9.9 %collective-permute-start.10 = (bf16[128,1152]{1,0:T(8,128)(2,1)S(1)}, bf16[128,1152]{1,0:T(8,128)(2,1)S(1)}, u32[]{:S(2)}, u32[]{:S(2)}) collective-permute-start(bf16[128,1152]{1,0:T(8,128)(2,1)S(1)} %get-tuple-element.31), channel_id=1, source_target_pairs={{0,4},{1,5},{2,6},{3,7},{16,20},{17,21},{18,22},{19,23},{8,12},{9,... | collective-permute-start | bytes 884744 | tf_op jit(solution)/shard_map/ppermute | solution.py:381
  26.5 9.5 %collective-permute-start.9 = (bf16[128,1152]{1,0:T(8,128)(2,1)S(1)}, bf16[128,1152]{1,0:T(8,128)(2,1)S(1)}, u32[]{:S(2)}, u32[]{:S(2)}) collective-permute-start(bf16[128,1152]{1,0:T(8,128)(2,1)S(1)} %get-tuple-element.31), channel_id=1, source_target_pairs={{0,20},{1,21},{2,22},{3,23},{16,4},{17,5},{18,6},{19,7},{8,28},{9,... | collective-permute-start | bytes 884744 | tf_op jit(solution)/shard_map/ppermute | solution.py:381
  27.8 94.0 %collective-permute-start.42 = (bf16[1,2048,512]{2,1,0:T(8,128)(2,1)}, bf16[1,2048,512]{2,1,0:T(8,128)(2,1)}, u32[]{:S(2)}, u32[]{:S(2)}) collective-permute-start(bf16[1,2048,512]{2,1,0:T(8,128)(2,1)} %param.11), channel_id=1, source_target_pairs={{12,24},{13,25},{14,26},{15,27},{28,8},{29,9},{30,10},{31,11}} | collective-permute-start | bytes 6291464 | tf_op jit(solution)/shard_map/ppermute | solution.py:381
  59.4 34.5 %collective-permute-start.30 = (bf16[128,1152]{1,0:T(8,128)(2,1)S(1)}, bf16[128,1152]{1,0:T(8,128)(2,1)S(1)}, u32[]{:S(2)}, u32[]{:S(2)}) collective-permute-start(bf16[128,1152]{1,0:T(8,128)(2,1)S(1)} %get-tuple-element.43), channel_id=1, source_target_pairs={{0,20},{1,21},{2,22},{3,23},{16,4},{17,5},{18,6},{19,7},{8,28},{9,... | collective-permute-start | bytes 884744 | tf_op jit(solution)/shard_map/ppermute | solution.py:381
  60.7 33.2 %collective-permute-start.31 = (bf16[128,1152]{1,0:T(8,128)(2,1)S(1)}, bf16[128,1152]{1,0:T(8,128)(2,1)S(1)}, u32[]{:S(2)}, u32[]{:S(2)}) collective-permute-start(bf16[128,1152]{1,0:T(8,128)(2,1)S(1)} %get-tuple-element.43), channel_id=1, source_target_pairs={{0,4},{1,5},{2,6},{3,7},{16,20},{17,21},{18,22},{19,23},{8,12},{9,... | collective-permute-start | bytes 884744 | tf_op jit(solution)/shard_map/ppermute | solution.py:381
  95.7 5.4 %collective-permute-start.32 = (bf16[128,512]{1,0:T(8,128)(2,1)S(1)}, bf16[128,512]{1,0:T(8,128)(2,1)S(1)}, u32[]{:S(2)}, u32[]{:S(2)}) collective-permute-start(bf16[128,512]{1,0:T(8,128)(2,1)S(1)} %get-tuple-element.44), channel_id=1, source_target_pairs={{12,10},{13,11},{14,8},{15,9},{28,26},{29,27},{30,24},{31,25}} | collective-permute-start | bytes 393224 | tf_op jit(solution)/shard_map/ppermute | solution.py:381
  98.3 5.8 %collective-permute-start.34 = (bf16[128,512]{1,0:T(8,128)(2,1)S(1)}, bf16[128,512]{1,0:T(8,128)(2,1)S(1)}, u32[]{:S(2)}, u32[]{:S(2)}) collective-permute-start(bf16[128,512]{1,0:T(8,128)(2,1)S(1)} %get-tuple-element.46), channel_id=1, source_target_pairs={{12,11},{13,8},{14,9},{15,10},{28,27},{29,24},{30,25},{31,26}} | collective-permute-start | bytes 393224 | tf_op jit(solution)/shard_map/ppermute | solution.py:381
  104.1 7.7 %collective-permute-start.36 = (bf16[128,512]{1,0:T(8,128)(2,1)S(1)}, bf16[128,512]{1,0:T(8,128)(2,1)S(1)}, u32[]{:S(2)}, u32[]{:S(2)}) collective-permute-start(bf16[128,512]{1,0:T(8,128)(2,1)S(1)} %combine.5.refs_1_), channel_id=1, source_target_pairs={{8,14},{9,15},{10,12},{11,13},{24,30},{25,31},{26,28},{27,29}} | collective-permute-start | bytes 393224 | tf_op jit(solution)/shard_map/ppermute | solution.py:381
  105.4 6.6 %collective-permute-start.37 = (bf16[128,512]{1,0:T(8,128)(2,1)S(1)}, bf16[128,512]{1,0:T(8,128)(2,1)S(1)}, u32[]{:S(2)}, u32[]{:S(2)}) collective-permute-start(bf16[128,512]{1,0:T(8,128)(2,1)S(1)} %combine.5.refs_1_), channel_id=1, source_target_pairs={{8,13},{9,14},{10,15},{11,12},{24,29},{25,30},{26,31},{27,28}} | collective-permute-start | bytes 393224 | tf_op jit(solution)/shard_map/ppermute | solution.py:381
  106.7 7.8 %collective-permute-start.38 = (bf16[128,512]{1,0:T(8,128)(2,1)S(1)}, bf16[128,512]{1,0:T(8,128)(2,1)S(1)}, u32[]{:S(2)}, u32[]{:S(2)}) collective-permute-start(bf16[128,512]{1,0:T(8,128)(2,1)S(1)} %combine.5.refs_1_), channel_id=1, source_target_pairs={{8,15},{9,12},{10,13},{11,14},{24,31},{25,28},{26,29},{27,30}} | collective-permute-start | bytes 393224 | tf_op jit(solution)/shard_map/ppermute | solution.py:381
  108.0 6.5 %collective-permute-start.39 = (bf16[128,512]{1,0:T(8,128)(2,1)S(1)}, bf16[128,512]{1,0:T(8,128)(2,1)S(1)}, u32[]{:S(2)}, u32[]{:S(2)}) collective-permute-start(bf16[128,512]{1,0:T(8,128)(2,1)S(1)} %combine.5.refs_1_), channel_id=1, source_target_pairs={{0,4},{1,5},{2,6},{3,7},{16,20},{17,21},{18,22},{19,23},{8,12},{9,... | collective-permute-start | bytes 393224 | tf_op jit(solution)/shard_map/ppermute | solution.py:381
  115.4 5.8 %collective-permute-start.47 = (bf16[64,1024]{1,0:T(8,128)(2,1)S(1)}, bf16[64,1024]{1,0:T(8,128)(2,1)S(1)}, u32[]{:S(2)}, u32[]{:S(2)}) collective-permute-start(bf16[64,1024]{1,0:T(8,128)(2,1)S(1)} %get-tuple-element.55), channel_id=1, source_target_pairs={{12,28},{13,29},{30,14},{31,15}} | collective-permute-start | bytes 393224 | tf_op jit(solution)/shard_map/ppermute | solution.py:381
  120.5 5.4 %collective-permute-start.49 = (bf16[64,512]{1,0:T(8,128)(2,1)S(1)}, bf16[64,512]{1,0:T(8,128)(2,1)S(1)}, u32[]{:S(2)}, u32[]{:S(2)}) collective-permute-start(bf16[64,512]{1,0:T(8,128)(2,1)S(1)} %get-tuple-element.58), channel_id=1, source_target_pairs={{0,0},{1,16},{2,1},{3,17},{16,2},{17,18},{18,3},{19,19},{4,4},{5,2... | collective-permute-start | bytes 196616 | tf_op jit(solution)/shard_map/ppermute | solution.py:381
  121.2 6.0 %collective-permute-start.50 = (bf16[64,512]{1,0:T(8,128)(2,1)S(1)}, bf16[64,512]{1,0:T(8,128)(2,1)S(1)}, u32[]{:S(2)}, u32[]{:S(2)}) collective-permute-start(bf16[64,512]{1,0:T(8,128)(2,1)S(1)} %get-tuple-element.57), channel_id=1, source_target_pairs={{0,16},{1,0},{2,17},{3,1},{16,18},{17,2},{18,19},{19,3},{4,20},{5,... | collective-permute-start | bytes 196616 | tf_op jit(solution)/shard_map/ppermute | solution.py:381
  121.9 6.6 %collective-permute-start.48 = (bf16[64,1024]{1,0:T(8,128)(2,1)S(1)}, bf16[64,1024]{1,0:T(8,128)(2,1)S(1)}, u32[]{:S(2)}, u32[]{:S(2)}) collective-permute-start(bf16[64,1024]{1,0:T(8,128)(2,1)S(1)} %broadcast_select_fusion.refs_4_), channel_id=1, source_target_pairs={{4,0},{5,1},{6,2},{7,3},{20,16},{21,17},{22,18},{23,19},{12,8},{13... | collective-permute-start | bytes 393224 | tf_op jit(solution)/shard_map/ppermute | solution.py:381
  123.2 9.2 %collective-permute-start.43 = (bf16[64,1024]{1,0:T(8,128)(2,1)S(1)}, bf16[64,1024]{1,0:T(8,128)(2,1)S(1)}, u32[]{:S(2)}, u32[]{:S(2)}) collective-permute-start(bf16[64,1024]{1,0:T(8,128)(2,1)S(1)} %get-tuple-element.50), channel_id=1, source_target_pairs={{8,14},{9,15},{10,12},{11,13},{24,30},{25,31},{26,28},{27,29}} | collective-permute-start | bytes 393224 | tf_op jit(solution)/shard_map/ppermute | solution.py:381
  124.5 7.9 %collective-permute-start.44 = (bf16[64,1024]{1,0:T(8,128)(2,1)S(1)}, bf16[64,1024]{1,0:T(8,128)(2,1)S(1)}, u32[]{:S(2)}, u32[]{:S(2)}) collective-permute-start(bf16[64,1024]{1,0:T(8,128)(2,1)S(1)} %get-tuple-element.51), channel_id=1, source_target_pairs={{8,13},{9,14},{10,15},{11,12},{24,29},{25,30},{26,31},{27,28}} | collective-permute-start | bytes 393224 | tf_op jit(solution)/shard_map/ppermute | solution.py:381
  125.8 10.3 %collective-permute-start.45 = (bf16[64,1024]{1,0:T(8,128)(2,1)S(1)}, bf16[64,1024]{1,0:T(8,128)(2,1)S(1)}, u32[]{:S(2)}, u32[]{:S(2)}) collective-permute-start(bf16[64,1024]{1,0:T(8,128)(2,1)S(1)} %get-tuple-element.52), channel_id=1, source_target_pairs={{8,15},{9,12},{10,13},{11,14},{24,31},{25,28},{26,29},{27,30}} | collective-permute-start | bytes 393224 | tf_op jit(solution)/shard_map/ppermute | solution.py:381
  127.2 9.0 %collective-permute-start.46 = (bf16[64,1024]{1,0:T(8,128)(2,1)S(1)}, bf16[64,1024]{1,0:T(8,128)(2,1)S(1)}, u32[]{:S(2)}, u32[]{:S(2)}) collective-permute-start(bf16[64,1024]{1,0:T(8,128)(2,1)S(1)} %get-tuple-element.53), channel_id=1, source_target_pairs={{0,4},{1,5},{2,6},{3,7},{16,20},{17,21},{18,22},{19,23},{8,12},{9,... | collective-permute-start | bytes 393224 | tf_op jit(solution)/shard_map/ppermute | solution.py:381
  (33 other events, 153.2 us)

commit v2 on v1

--- a/solution.py
+++ b/solution.py
@@ -192,6 +192,25 @@
     )(weight, after)
 
 
+def turn_kernel(weight, after, out, held, sem):
+    copy = pltpu.make_async_copy(weight, held, sem)
+    copy.start()
+    copy.wait()
+    out[...] = held[0].T
+
+
+def turned(section, weight, after):
+    return pl.pallas_call(
+        on_section(turn_kernel, section),
+        out_shape=jax.ShapeDtypeStruct(weight.shape[:0:-1], weight.dtype),
+        in_specs=[HBM, ANY],
+        out_specs=VMEM,
+        scratch_shapes=[pltpu.VMEM(weight.shape, weight.dtype), pltpu.SemaphoreType.DMA],
+        name="turn",
+        compiler_params=pltpu.CompilerParams(vmem_limit_bytes=8 << 20),
+    )(weight, after)
+
+
 def attended_heads(total, inverse, cosine, sine, block, query_heads, key_value_heads, only):
     rows = total.shape[0]
     asked = rows if only is None else block
@@ -248,39 +267,29 @@
     return lax.dot_general(left, right, (((1,), (1,)), ((), ())), preferred_element_type=jnp.float32)
 
 
-def attend_kernel(got, mine, cosine, sine, lent, *refs, ways, block, features, heads):
-    outs, (weight, sem) = refs[:ways], refs[ways:]
-    copy = pltpu.make_async_copy(lent, weight, sem)
-    copy.start()
+def attend_kernel(got, mine, cosine, sine, weight, *outs, ways, block, features, heads):
     rank = lax.axis_index("tp")
-    width = weight.shape[1] // ways
+    width = outs[0].shape[1]
     total, inverse = summed(got, mine, features)
     attended = attended_heads(total, inverse, cosine[...], sine[...], block, *heads, None)
-    copy.wait()
     for k in range(ways):
         first = pl.multiple_of(lax.rem(rank + k, ways) * width, width)
-        outs[k][...] = times_transposed(attended, weight[0, pl.ds(first, width), :]).astype(outs[k].dtype)
-
-
-def last_kernel(got, mine, cosine, sine, lent, far_weight, *refs, ways, block, features, heads):
-    outs, (weight, sem, other_weight, other_sem, slots) = refs[:ways], refs[ways:]
+        product = jnp.dot(attended, weight[:, pl.ds(first, width)], preferred_element_type=jnp.float32)
+        outs[k][...] = product.astype(outs[k].dtype)
+
+
+def last_kernel(got, mine, cosine, sine, weight, other_weight, *refs, ways, block, features, heads):
+    outs, (slots,) = refs[:ways], refs[ways:]
     rank, group = lax.axis_index("tp"), lax.axis_index("seq")
     width = outs[0].shape[1]
-    copies = [
-        pltpu.make_async_copy(lent, weight, sem),
-        pltpu.make_async_copy(far_weight, other_weight, other_sem),
-    ]
-    for copy in copies:
-        copy.start()
     total, inverse = summed(got, mine, features)
     attended = attended_heads(total, inverse, cosine[...], sine[...], block, *heads, group)
     per_half = weight.shape[1] // width
-    for side, held, copy in ((group, weight, copies[0]), (1 - group, other_weight, copies[1])):
-        copy.wait()
+    for side, held in ((group, weight), (1 - group, other_weight)):
         for i in range(per_half):
             shift = lax.rem(side * per_half + i + ways - rank, ways)
-            product = times_transposed(attended, held[0, i * width : (i + 1) * width, :])
-            slots[shift] = product.astype(slots.dtype)
+            columns = held[:, i * width : (i + 1) * width]
+            slots[shift] = jnp.dot(attended, columns, preferred_element_type=jnp.float32).astype(slots.dtype)
     for k in range(ways):
         outs[k][...] = slots[k]
 
@@ -296,16 +305,11 @@
             section,
         ),
         out_shape=[jax.ShapeDtypeStruct(shape, jnp.bfloat16) for _ in range(ways)],
-        in_specs=[VMEM] * 4 + [HBM] * len(weights),
+        in_specs=[VMEM] * (4 + len(weights)),
         out_specs=[VMEM] * ways,
-        scratch_shapes=[
-            scratch
-            for weight in weights
-            for scratch in (pltpu.VMEM(weight.shape, jnp.bfloat16), pltpu.SemaphoreType.DMA)
-        ]
-        + ([pltpu.VMEM((ways,) + shape, jnp.bfloat16)] if last else []),
+        scratch_shapes=[pltpu.VMEM((ways,) + shape, jnp.bfloat16)] if last else [],
         name="attend",
-        compiler_params=pltpu.CompilerParams(vmem_limit_bytes=8 << 20),
+        compiler_params=pltpu.CompilerParams(vmem_limit_bytes=6 << 20),
     )(got, mine, cosine, sine, *weights)
 
 
@@ -405,6 +409,7 @@
                 pairs.append((at(b % seq_count, servers[group](t1), b // seq_count), at(s1, 0, t1)))
             arrivals[k, group] = moved(looked, pairs)
     staged = stage(0, qkv_weight, looked)
+    out_turned = [turned(partner(0), lent, looked)]
     pieces = [arrivals[k, group] for k in send_order(ways) for group in range(2)]
 
     def shifted(source, target, k):
@@ -437,10 +442,12 @@
         got_near = moved(message, shifted(layer, aside, 0))
         if layer == end:
             break
-        outs = attend(aside, got_far, got_near, cosine, sine, [lent], ways, block, features, heads)
+        outs = attend(aside, got_far, got_near, cosine, sine, out_turned, ways, block, features, heads)
         parts = [moved(outs[k], shifted(aside, layer, k)) for k in send_order(ways)]
         fresh = combine(parts, kept[0])
         staged = stage(layer + 1, qkv_weight, fresh)
+        lenders = [lent, lent_far] if layer + 1 == end else [lent]
+        out_turned = [turned(partner(layer + 1), weight, fresh) for weight in lenders]
         if layer < end - 1:
             state = jnp.where(c == layer, fresh, state)
         pieces = [moved(fresh, shifted(layer, layer + 1, k)) for k in send_order(ways)]
@@ -448,7 +455,7 @@
     mine, other = kept
     brought = moved(other, [(at(t1 // 2, end, t1), at(1 - t1 // 2, end, t1)) for t1 in range(ways)])
     residual = jnp.where(s == t // 2, mine, brought)
-    outs = attend(aside, got_far, got_near, cosine, sine, [lent, lent_far], ways, block, features, heads)
+    outs = attend(aside, got_far, got_near, cosine, sine, out_turned, ways, block, features, heads)
     parts = []
     for k in send_order(ways):
         parts.append(moved(outs[k], shifted(partner(end), end, k)))

time: 138 us -> 139 us (level)
  the two profiles are of different devices: /device:TPU:11 before, /device:TPU:3 now
where the time goes in v2:
time: 139 us; the launch traced here: 138 us
  starting transfers between devices  61 us (44%)
  waiting for transfers between devices  59.3 us (43%)
  Pallas kernels  12 us (9%)
  local copies, waits for them, and re-layouts  4.41 us (3%)
    ppermute x49, starting transfers between devices, moved(): return lax.ppermute(value, AXES, pairs)  59.1 us
    ppermute x49, waiting for transfers between devices, moved(): return lax.ppermute(value, AXES, pairs)  58 us
    pallas_call x1, Pallas kernels, lookup(): pl.pallas_call(lookup_kernel, out_shape=jax.ShapeDtypeStruct((count, feat...  7.73 us
    unnamed x12, local copies, waits for them, and re-layouts  4.39 us
  transfers between devices with their start and end apart: 51, of which 14 were waited for; matrix products, arithmetic and copies ran while one was open for 0% of the time, Pallas kernels for 8%

profile of v2, /device:TPU:3, one launch (start us, length us, event | category | flops | bytes accessed | tf_op | source)
XLA Modules:
  0.0 137.7 jit_solution(2433461618307350836)
XLA Ops:
  1.9 1.3 collective-permute-done
  3.2 7.7 %lookup.1.refs_1_ = bf16[64,512]{1,0:T(8,128)(2,1)S(1)} custom-call(s32[64]{0:T(128)S(1)} %broadcast_select_fusion.1.ids_smem, s32[1,64]{1,0:T(1,128)S(1)} %bitcast.1, bf16[512,65536]{1,0:T(8,128)(2,1)} %table.1), custom_call_target="tpu_custom_call" | custom-call | tf_op jit(solution)/shard_map/lookup/pallas_call | solution.py:98
  11.7 1.3 collective-permute-start.2
  15.0 4.9 %collective-permute-start.42 = (bf16[1,2048,512]{2,1,0:T(8,128)(2,1)}, bf16[1,2048,512]{2,1,0:T(8,128)(2,1)}, u32[]{:S(2)}, u32[]{:S(2)}) collective-permute-start(bf16[1,2048,512]{2,1,0:T(8,128)(2,1)} %param.11), channel_id=1, source_target_pairs={{12,24},{13,25},{14,26},{15,27},{28,8},{29,9},{30,10},{31,11}} | collective-permute-start | bytes 6291464 | tf_op jit(solution)/shard_map/ppermute | solution.py:385
  19.9 4.7 %collective-permute-start.6 = (bf16[64,512]{1,0:T(8,128)(2,1)S(1)}, bf16[64,512]{1,0:T(8,128)(2,1)S(1)}, u32[]{:S(2)}, u32[]{:S(2)}) collective-permute-start(bf16[64,512]{1,0:T(8,128)(2,1)S(1)} %lookup.1.refs_1_), channel_id=1, source_target_pairs={{24,0},{9,1},{29,2},{12,3},{26,16},{11,17},{31,18},{14,19}} | collective-permute-start | bytes 196616 | tf_op jit(solution)/shard_map/ppermute | solution.py:385
  26.0 2.2 %copy-done = bf16[1,2048,1024]{2,1,0:T(8,128)(2,1)S(1)} copy-done((bf16[1,2048,1024]{2,1,0:T(8,128)(2,1)S(1)}, bf16[1,2048,1024]{2,1,0:T(8,128)(2,1)}, u32[]{:S(2)}) %copy-start) | copy-done | bytes 4194328
  28.3 1.4 %collective-permute-start.10 = (bf16[128,1152]{1,0:T(8,128)(2,1)S(1)}, bf16[128,1152]{1,0:T(8,128)(2,1)S(1)}, u32[]{:S(2)}, u32[]{:S(2)}) collective-permute-start(bf16[128,1152]{1,0:T(8,128)(2,1)S(1)} %get-tuple-element.31), channel_id=1, source_target_pairs={{0,4},{1,5},{2,6},{3,7},{16,20},{17,21},{18,22},{19,23},{8,12},{9,... | collective-permute-start | bytes 884744 | tf_op jit(solution)/shard_map/ppermute | solution.py:385
  31.9 9.4 %collective-permute-done.9.refs_0_ = bf16[128,1152]{1,0:T(8,128)(2,1)S(1)} collective-permute-done((bf16[128,1152]{1,0:T(8,128)(2,1)S(1)}, bf16[128,1152]{1,0:T(8,128)(2,1)S(1)}, u32[]{:S(2)}, u32[]{:S(2)}) %collective-permute-start.9) | collective-permute-done | bytes 294944 | tf_op jit(solution)/shard_map/ppermute | solution.py:385
  43.3 1.3 collective-permute-start.15
  49.1 1.9 %collective-permute-done.19.refs_3_ = bf16[128,512]{1,0:T(8,128)(2,1)S(1)} collective-permute-done((bf16[128,512]{1,0:T(8,128)(2,1)S(1)}, bf16[128,512]{1,0:T(8,128)(2,1)S(1)}, u32[]{:S(2)}, u32[]{:S(2)}) %collective-permute-start.19) | collective-permute-done | bytes 131104 | tf_op jit(solution)/shard_map/ppermute | solution.py:385
  51.7 2.1 %collective-permute-start.21 = (bf16[128,1152]{1,0:T(8,128)(2,1)S(1)}, bf16[128,1152]{1,0:T(8,128)(2,1)S(1)}, u32[]{:S(2)}, u32[]{:S(2)}) collective-permute-start(bf16[128,1152]{1,0:T(8,128)(2,1)S(1)} %get-tuple-element.37), channel_id=1, source_target_pairs={{4,0},{5,1},{6,2},{7,3},{20,16},{21,17},{22,18},{23,19},{12,8},{13... | collective-permute-start | bytes 884744 | tf_op jit(solution)/shard_map/ppermute | solution.py:385
  58.3 1.9 %collective-permute-done.25.refs_3_ = bf16[128,512]{1,0:T(8,128)(2,1)S(1)} collective-permute-done((bf16[128,512]{1,0:T(8,128)(2,1)S(1)}, bf16[128,512]{1,0:T(8,128)(2,1)S(1)}, u32[]{:S(2)}, u32[]{:S(2)}) %collective-permute-start.25) | collective-permute-done | bytes 131104 | tf_op jit(solution)/shard_map/ppermute | solution.py:385
  66.5 30.9 %collective-permute-done.30.refs_0_ = bf16[128,1152]{1,0:T(8,128)(2,1)S(1)} collective-permute-done((bf16[128,1152]{1,0:T(8,128)(2,1)S(1)}, bf16[128,1152]{1,0:T(8,128)(2,1)S(1)}, u32[]{:S(2)}, u32[]{:S(2)}) %collective-permute-start.30) | collective-permute-done | bytes 294944 | tf_op jit(solution)/shard_map/ppermute | solution.py:385
  98.5 1.3 collective-permute-start.32
  99.8 1.3 collective-permute-start.33
  101.1 1.3 collective-permute-start.34
  102.4 1.3 collective-permute-start.35
  110.0 2.2 %copy-done.2 = bf16[1,2048,1024]{2,1,0:T(8,128)(2,1)S(1)} copy-done((bf16[1,2048,1024]{2,1,0:T(8,128)(2,1)S(1)}, bf16[1,2048,1024]{2,1,0:T(8,128)(2,1)}, u32[]{:S(2)}) %copy-start.2) | copy-done | bytes 4194328
  112.5 2.5 %collective-permute-done.37.refs_1_ = bf16[128,512]{1,0:T(8,128)(2,1)S(1)} collective-permute-done((bf16[128,512]{1,0:T(8,128)(2,1)S(1)}, bf16[128,512]{1,0:T(8,128)(2,1)S(1)}, u32[]{:S(2)}, u32[]{:S(2)}) %collective-permute-start.37) | collective-permute-done | bytes 131104 | tf_op jit(solution)/shard_map/ppermute | solution.py:385
  116.7 2.7 %collective-permute-start.47 = (bf16[64,1024]{1,0:T(8,128)(2,1)S(1)}, bf16[64,1024]{1,0:T(8,128)(2,1)S(1)}, u32[]{:S(2)}, u32[]{:S(2)}) collective-permute-start(bf16[64,1024]{1,0:T(8,128)(2,1)S(1)} %get-tuple-element.55), channel_id=1, source_target_pairs={{12,28},{13,29},{30,14},{31,15}} | collective-permute-start | bytes 393224 | tf_op jit(solution)/shard_map/ppermute | solution.py:385
  119.4 1.3 collective-permute-start.40
  120.7 1.3 collective-permute-start.41
  123.5 1.4 %collective-permute-start.48 = (bf16[64,1024]{1,0:T(8,128)(2,1)S(1)}, bf16[64,1024]{1,0:T(8,128)(2,1)S(1)}, u32[]{:S(2)}, u32[]{:S(2)}) collective-permute-start(bf16[64,1024]{1,0:T(8,128)(2,1)S(1)} %broadcast_select_fusion.refs_4_), channel_id=1, source_target_pairs={{4,0},{5,1},{6,2},{7,3},{20,16},{21,17},{22,18},{23,19},{12,8},{13... | collective-permute-start | bytes 393224 | tf_op jit(solution)/shard_map/ppermute | solution.py:385
  130.2 5.7 %collective-permute-done.43.refs_0_ = bf16[64,1024]{1,0:T(8,128)(2,1)S(1)} collective-permute-done((bf16[64,1024]{1,0:T(8,128)(2,1)S(1)}, bf16[64,1024]{1,0:T(8,128)(2,1)S(1)}, u32[]{:S(2)}, u32[]{:S(2)}) %collective-permute-start.43) | collective-permute-done | bytes 131104 | tf_op jit(solution)/shard_map/ppermute | solution.py:385
  (117 shorter events, 43.5 us)
Async XLA Ops:
  0.0 31.0 %collective-permute-start.11 = (bf16[1,2048,512]{2,1,0:T(8,128)(2,1)}, bf16[1,2048,512]{2,1,0:T(8,128)(2,1)S(1)}, u32[]{:S(2)}, u32[]{:S(2)}) collective-permute-start(bf16[1,2048,512]{2,1,0:T(8,128)(2,1)} %param.11), channel_id=1, source_target_pairs={{0,4},{4,0},{8,12},{12,8},{1,5},{5,1},{9,13},{13,9},{2,6},{6,2},{1... | collective-permute-start | bytes 6291464 | tf_op jit(solution)/shard_map/ppermute | solution.py:395
  13.0 7.0 %collective-permute-start.3 = (bf16[64,512]{1,0:T(8,128)(2,1)S(1)}, bf16[64,512]{1,0:T(8,128)(2,1)S(1)}, u32[]{:S(2)}, u32[]{:S(2)}) collective-permute-start(bf16[64,512]{1,0:T(8,128)(2,1)S(1)} %lookup.1.refs_1_), channel_id=1, source_target_pairs={{21,0},{4,1},{20,2},{5,3},{23,16},{6,17},{22,18},{7,19}} | collective-permute-start | bytes 196616 | tf_op jit(solution)/shard_map/ppermute | solution.py:385
  13.6 11.0 %collective-permute-start.4 = (bf16[64,512]{1,0:T(8,128)(2,1)S(1)}, bf16[64,512]{1,0:T(8,128)(2,1)S(1)}, u32[]{:S(2)}, u32[]{:S(2)}) collective-permute-start(bf16[64,512]{1,0:T(8,128)(2,1)S(1)} %lookup.1.refs_1_), channel_id=1, source_target_pairs={{25,0},{8,1},{28,2},{13,3},{27,16},{10,17},{30,18},{15,19}} | collective-permute-start | bytes 196616 | tf_op jit(solution)/shard_map/ppermute | solution.py:385
  14.3 11.0 %collective-permute-start.5 = (bf16[64,512]{1,0:T(8,128)(2,1)S(1)}, bf16[64,512]{1,0:T(8,128)(2,1)S(1)}, u32[]{:S(2)}, u32[]{:S(2)}) collective-permute-start(bf16[64,512]{1,0:T(8,128)(2,1)S(1)} %lookup.1.refs_1_), channel_id=1, source_target_pairs={{20,0},{5,1},{21,2},{4,3},{22,16},{7,17},{23,18},{6,19}} | collective-permute-start | bytes 196616 | tf_op jit(solution)/shard_map/ppermute | solution.py:385
  15.0 107.8 %collective-permute-start.42 = (bf16[1,2048,512]{2,1,0:T(8,128)(2,1)}, bf16[1,2048,512]{2,1,0:T(8,128)(2,1)}, u32[]{:S(2)}, u32[]{:S(2)}) collective-permute-start(bf16[1,2048,512]{2,1,0:T(8,128)(2,1)} %param.11), channel_id=1, source_target_pairs={{12,24},{13,25},{14,26},{15,27},{28,8},{29,9},{30,10},{31,11}} | collective-permute-start | bytes 6291464 | tf_op jit(solution)/shard_map/ppermute | solution.py:385
  19.9 8.3 %collective-permute-start.6 = (bf16[64,512]{1,0:T(8,128)(2,1)S(1)}, bf16[64,512]{1,0:T(8,128)(2,1)S(1)}, u32[]{:S(2)}, u32[]{:S(2)}) collective-permute-start(bf16[64,512]{1,0:T(8,128)(2,1)S(1)} %lookup.1.refs_1_), channel_id=1, source_target_pairs={{24,0},{9,1},{29,2},{12,3},{26,16},{11,17},{31,18},{14,19}} | collective-permute-start | bytes 196616 | tf_op jit(solution)/shard_map/ppermute | solution.py:385
  29.7 11.6 %collective-permute-start.9 = (bf16[128,1152]{1,0:T(8,128)(2,1)S(1)}, bf16[128,1152]{1,0:T(8,128)(2,1)S(1)}, u32[]{:S(2)}, u32[]{:S(2)}) collective-permute-start(bf16[128,1152]{1,0:T(8,128)(2,1)S(1)} %get-tuple-element.31), channel_id=1, source_target_pairs={{0,20},{1,21},{2,22},{3,23},{16,4},{17,5},{18,6},{19,7},{8,28},{9,... | collective-permute-start | bytes 884744 | tf_op jit(solution)/shard_map/ppermute | solution.py:385
  63.1 34.3 %collective-permute-start.30 = (bf16[128,1152]{1,0:T(8,128)(2,1)S(1)}, bf16[128,1152]{1,0:T(8,128)(2,1)S(1)}, u32[]{:S(2)}, u32[]{:S(2)}) collective-permute-start(bf16[128,1152]{1,0:T(8,128)(2,1)S(1)} %get-tuple-element.43), channel_id=1, source_target_pairs={{0,20},{1,21},{2,22},{3,23},{16,4},{17,5},{18,6},{19,7},{8,28},{9,... | collective-permute-start | bytes 884744 | tf_op jit(solution)/shard_map/ppermute | solution.py:385
  64.4 33.0 %collective-permute-start.31 = (bf16[128,1152]{1,0:T(8,128)(2,1)S(1)}, bf16[128,1152]{1,0:T(8,128)(2,1)S(1)}, u32[]{:S(2)}, u32[]{:S(2)}) collective-permute-start(bf16[128,1152]{1,0:T(8,128)(2,1)S(1)} %get-tuple-element.43), channel_id=1, source_target_pairs={{0,4},{1,5},{2,6},{3,7},{16,20},{17,21},{18,22},{19,23},{8,12},{9,... | collective-permute-start | bytes 884744 | tf_op jit(solution)/shard_map/ppermute | solution.py:385
  98.5 5.2 %collective-permute-start.32 = (bf16[128,512]{1,0:T(8,128)(2,1)S(1)}, bf16[128,512]{1,0:T(8,128)(2,1)S(1)}, u32[]{:S(2)}, u32[]{:S(2)}) collective-permute-start(bf16[128,512]{1,0:T(8,128)(2,1)S(1)} %get-tuple-element.44), channel_id=1, source_target_pairs={{12,10},{13,11},{14,8},{15,9},{28,26},{29,27},{30,24},{31,25}} | collective-permute-start | bytes 393224 | tf_op jit(solution)/shard_map/ppermute | solution.py:385
  104.8 7.7 %collective-permute-start.36 = (bf16[128,512]{1,0:T(8,128)(2,1)S(1)}, bf16[128,512]{1,0:T(8,128)(2,1)S(1)}, u32[]{:S(2)}, u32[]{:S(2)}) collective-permute-start(bf16[128,512]{1,0:T(8,128)(2,1)S(1)} %combine.5.refs_1_), channel_id=1, source_target_pairs={{8,14},{9,15},{10,12},{11,13},{24,30},{25,31},{26,28},{27,29}} | collective-permute-start | bytes 393224 | tf_op jit(solution)/shard_map/ppermute | solution.py:385
  106.1 8.9 %collective-permute-start.37 = (bf16[128,512]{1,0:T(8,128)(2,1)S(1)}, bf16[128,512]{1,0:T(8,128)(2,1)S(1)}, u32[]{:S(2)}, u32[]{:S(2)}) collective-permute-start(bf16[128,512]{1,0:T(8,128)(2,1)S(1)} %combine.5.refs_1_), channel_id=1, source_target_pairs={{8,13},{9,14},{10,15},{11,12},{24,29},{25,30},{26,31},{27,28}} | collective-permute-start | bytes 393224 | tf_op jit(solution)/shard_map/ppermute | solution.py:385
  107.4 8.5 %collective-permute-start.38 = (bf16[128,512]{1,0:T(8,128)(2,1)S(1)}, bf16[128,512]{1,0:T(8,128)(2,1)S(1)}, u32[]{:S(2)}, u32[]{:S(2)}) collective-permute-start(bf16[128,512]{1,0:T(8,128)(2,1)S(1)} %combine.5.refs_1_), channel_id=1, source_target_pairs={{8,15},{9,12},{10,13},{11,14},{24,31},{25,28},{26,29},{27,30}} | collective-permute-start | bytes 393224 | tf_op jit(solution)/shard_map/ppermute | solution.py:385
  108.7 7.2 %collective-permute-start.39 = (bf16[128,512]{1,0:T(8,128)(2,1)S(1)}, bf16[128,512]{1,0:T(8,128)(2,1)S(1)}, u32[]{:S(2)}, u32[]{:S(2)}) collective-permute-start(bf16[128,512]{1,0:T(8,128)(2,1)S(1)} %combine.5.refs_1_), channel_id=1, source_target_pairs={{0,4},{1,5},{2,6},{3,7},{16,20},{17,21},{18,22},{19,23},{8,12},{9,... | collective-permute-start | bytes 393224 | tf_op jit(solution)/shard_map/ppermute | solution.py:385
  116.7 6.8 %collective-permute-start.47 = (bf16[64,1024]{1,0:T(8,128)(2,1)S(1)}, bf16[64,1024]{1,0:T(8,128)(2,1)S(1)}, u32[]{:S(2)}, u32[]{:S(2)}) collective-permute-start(bf16[64,1024]{1,0:T(8,128)(2,1)S(1)} %get-tuple-element.55), channel_id=1, source_target_pairs={{12,28},{13,29},{30,14},{31,15}} | collective-permute-start | bytes 393224 | tf_op jit(solution)/shard_map/ppermute | solution.py:385
  119.4 5.6 %collective-permute-start.40 = (bf16[128,1152]{1,0:T(8,128)(2,1)S(1)}, bf16[128,1152]{1,0:T(8,128)(2,1)S(1)}, u32[]{:S(2)}, u32[]{:S(2)}) collective-permute-start(bf16[128,1152]{1,0:T(8,128)(2,1)S(1)} %get-tuple-element.49), channel_id=1, source_target_pairs={{12,24},{13,25},{14,26},{15,27},{28,8},{29,9},{30,10},{31,11}} | collective-permute-start | bytes 884744 | tf_op jit(solution)/shard_map/ppermute | solution.py:385
  120.7 4.2 %collective-permute-start.41 = (bf16[128,1152]{1,0:T(8,128)(2,1)S(1)}, bf16[128,1152]{1,0:T(8,128)(2,1)S(1)}, u32[]{:S(2)}, u32[]{:S(2)}) collective-permute-start(bf16[128,1152]{1,0:T(8,128)(2,1)S(1)} %get-tuple-element.49), channel_id=1, source_target_pairs={{4,0},{5,1},{6,2},{7,3},{20,16},{21,17},{22,18},{23,19},{12,8},{13... | collective-permute-start | bytes 884744 | tf_op jit(solution)/shard_map/ppermute | solution.py:385
  122.1 5.5 %collective-permute-start.49 = (bf16[64,512]{1,0:T(8,128)(2,1)S(1)}, bf16[64,512]{1,0:T(8,128)(2,1)S(1)}, u32[]{:S(2)}, u32[]{:S(2)}) collective-permute-start(bf16[64,512]{1,0:T(8,128)(2,1)S(1)} %get-tuple-element.58), channel_id=1, source_target_pairs={{0,0},{1,16},{2,1},{3,17},{16,2},{17,18},{18,3},{19,19},{4,4},{5,2... | collective-permute-start | bytes 196616 | tf_op jit(solution)/shard_map/ppermute | solution.py:385
  122.8 6.1 %collective-permute-start.50 = (bf16[64,512]{1,0:T(8,128)(2,1)S(1)}, bf16[64,512]{1,0:T(8,128)(2,1)S(1)}, u32[]{:S(2)}, u32[]{:S(2)}) collective-permute-start(bf16[64,512]{1,0:T(8,128)(2,1)S(1)} %get-tuple-element.57), channel_id=1, source_target_pairs={{0,16},{1,0},{2,17},{3,1},{16,18},{17,2},{18,19},{19,3},{4,20},{5,... | collective-permute-start | bytes 196616 | tf_op jit(solution)/shard_map/ppermute | solution.py:385
  123.5 6.7 %collective-permute-start.48 = (bf16[64,1024]{1,0:T(8,128)(2,1)S(1)}, bf16[64,1024]{1,0:T(8,128)(2,1)S(1)}, u32[]{:S(2)}, u32[]{:S(2)}) collective-permute-start(bf16[64,1024]{1,0:T(8,128)(2,1)S(1)} %broadcast_select_fusion.refs_4_), channel_id=1, source_target_pairs={{4,0},{5,1},{6,2},{7,3},{20,16},{21,17},{22,18},{23,19},{12,8},{13... | collective-permute-start | bytes 393224 | tf_op jit(solution)/shard_map/ppermute | solution.py:385
  125.0 10.9 %collective-permute-start.43 = (bf16[64,1024]{1,0:T(8,128)(2,1)S(1)}, bf16[64,1024]{1,0:T(8,128)(2,1)S(1)}, u32[]{:S(2)}, u32[]{:S(2)}) collective-permute-start(bf16[64,1024]{1,0:T(8,128)(2,1)S(1)} %get-tuple-element.50), channel_id=1, source_target_pairs={{8,14},{9,15},{10,12},{11,13},{24,30},{25,31},{26,28},{27,29}} | collective-permute-start | bytes 393224 | tf_op jit(solution)/shard_map/ppermute | solution.py:385
  126.3 9.6 %collective-permute-start.44 = (bf16[64,1024]{1,0:T(8,128)(2,1)S(1)}, bf16[64,1024]{1,0:T(8,128)(2,1)S(1)}, u32[]{:S(2)}, u32[]{:S(2)}) collective-permute-start(bf16[64,1024]{1,0:T(8,128)(2,1)S(1)} %get-tuple-element.51), channel_id=1, source_target_pairs={{8,13},{9,14},{10,15},{11,12},{24,29},{25,30},{26,31},{27,28}} | collective-permute-start | bytes 393224 | tf_op jit(solution)/shard_map/ppermute | solution.py:385
  127.6 9.3 %collective-permute-start.45 = (bf16[64,1024]{1,0:T(8,128)(2,1)S(1)}, bf16[64,1024]{1,0:T(8,128)(2,1)S(1)}, u32[]{:S(2)}, u32[]{:S(2)}) collective-permute-start(bf16[64,1024]{1,0:T(8,128)(2,1)S(1)} %get-tuple-element.52), channel_id=1, source_target_pairs={{8,15},{9,12},{10,13},{11,14},{24,31},{25,28},{26,29},{27,30}} | collective-permute-start | bytes 393224 | tf_op jit(solution)/shard_map/ppermute | solution.py:385
  128.9 8.0 %collective-permute-start.46 = (bf16[64,1024]{1,0:T(8,128)(2,1)S(1)}, bf16[64,1024]{1,0:T(8,128)(2,1)S(1)}, u32[]{:S(2)}, u32[]{:S(2)}) collective-permute-start(bf16[64,1024]{1,0:T(8,128)(2,1)S(1)} %get-tuple-element.53), channel_id=1, source_target_pairs={{0,4},{1,5},{2,6},{3,7},{16,20},{17,21},{18,22},{19,23},{8,12},{9,... | collective-permute-start | bytes 393224 | tf_op jit(solution)/shard_map/ppermute | solution.py:385
  (33 other events, 146.1 us)

commit v3 on v2

--- a/solution.py
+++ b/solution.py
@@ -62,34 +62,25 @@
     features, _ = table.shape
     count = ids_row.shape[1]
 
-    def start(i, _):
+    group = 8
+    wide = group * LANES
+    for i in range(count):
         first = pl.multiple_of((ids_smem[i] // LANES) * LANES, LANES)
         pltpu.make_async_copy(
             table.at[:, pl.ds(first, LANES)],
-            strips.at[:, pl.ds(pl.multiple_of(i * LANES, LANES), LANES)],
-            sems.at[i],
+            strips.at[:, pl.ds(i * LANES, LANES)],
+            sems.at[i // group],
         ).start()
-        return 0
-
-    lax.fori_loop(0, count, start, 0)
     lanes = lax.rem(ids_row[...], LANES)
-    group = 8
     acc = jnp.zeros((features, count), jnp.float32)
-    wide = group * LANES
     rows = lax.broadcasted_iota(jnp.int32, (wide, count), 0)
     target = lax.broadcasted_iota(jnp.int32, (1, count), 1) * LANES + lanes
     for g in range(count // group):
-        onehot[g] = jnp.where(rows + g * wide == target, 1.0, 0.0).astype(jnp.bfloat16)
+        onehot[g] = jnp.where(rows == target - g * wide, 1.0, 0.0).astype(jnp.bfloat16)
     for g in range(count // group):
-        for i in range(g * group, (g + 1) * group):
-            pltpu.make_async_copy(
-                table.at[:, pl.ds(0, LANES)],
-                strips.at[:, pl.ds(i * LANES, LANES)],
-                sems.at[i],
-            ).wait()
-        acc = acc + jnp.dot(
-            strips[:, g * wide : (g + 1) * wide], onehot[g], preferred_element_type=jnp.float32
-        )
+        there = pl.ds(g * wide, wide)
+        pltpu.make_async_copy(table.at[:, pl.ds(0, wide)], strips.at[:, there], sems.at[g]).wait()
+        acc = acc + jnp.dot(strips[:, there], onehot[g], preferred_element_type=jnp.float32)
     out[...] = acc.T.astype(jnp.bfloat16)
 
 
@@ -103,7 +94,7 @@
         scratch_shapes=[
             pltpu.VMEM((features, count * LANES), jnp.bfloat16),
             pltpu.VMEM((count // 8, 8 * LANES, count), jnp.bfloat16),
-            pltpu.SemaphoreType.DMA((count,)),
+            pltpu.SemaphoreType.DMA((count // 8,)),
         ],
         name="lookup",
         compiler_params=pltpu.CompilerParams(vmem_limit_bytes=16 << 20),
@@ -450,7 +441,9 @@
         out_turned = [turned(partner(layer + 1), weight, fresh) for weight in lenders]
         if layer < end - 1:
             state = jnp.where(c == layer, fresh, state)
-        pieces = [moved(fresh, shifted(layer, layer + 1, k)) for k in send_order(ways)]
+        pieces = []
+        for k in send_order(ways):
+            pieces.append(moved(fresh, shifted(layer, layer + 1, k)))
 
     mine, other = kept
     brought = moved(other, [(at(t1 // 2, end, t1), at(1 - t1 // 2, end, t1)) for t1 in range(ways)])

time: 139 us -> 138 us (level)
  no operation moved by 1% of the time
where the time goes in v3:
time: 138 us; the launch traced here: 137 us
  starting transfers between devices  61.1 us (44%)
  waiting for transfers between devices  59.2 us (43%)
  Pallas kernels  11.4 us (8%)
  local copies, waits for them, and re-layouts  4.41 us (3%)
    ppermute x49, starting transfers between devices, moved(): return lax.ppermute(value, AXES, pairs)  59.2 us
    ppermute x49, waiting for transfers between devices, moved(): return lax.ppermute(value, AXES, pairs)  57.8 us
    pallas_call x1, Pallas kernels, lookup(): pl.pallas_call(lookup_kernel, out_shape=jax.ShapeDtypeStruct((count, feat...  7.14 us
    unnamed x12, local copies, waits for them, and re-layouts  4.39 us
  transfers between devices with their start and end apart: 51, of which 14 were waited for; matrix products, arithmetic and copies ran while one was open for 0% of the time, Pallas kernels for 8%

profile of v3, /device:TPU:3, one launch (start us, length us, event | category | flops | bytes accessed | tf_op | source)
XLA Modules:
  0.0 137.1 jit_solution(10645040397108519583)
XLA Ops:
  1.9 1.3 collective-permute-done
  3.2 7.1 %lookup.1.refs_1_ = bf16[64,512]{1,0:T(8,128)(2,1)S(1)} custom-call(s32[64]{0:T(128)S(1)} %broadcast_select_fusion.1.ids_smem, s32[1,64]{1,0:T(1,128)S(1)} %bitcast.1, bf16[512,65536]{1,0:T(8,128)(2,1)} %table.1), custom_call_target="tpu_custom_call" | custom-call | tf_op jit(solution)/shard_map/lookup/pallas_call | solution.py:89
  11.1 1.3 collective-permute-start.2
  14.4 4.9 %collective-permute-start.42 = (bf16[1,2048,512]{2,1,0:T(8,128)(2,1)}, bf16[1,2048,512]{2,1,0:T(8,128)(2,1)}, u32[]{:S(2)}, u32[]{:S(2)}) collective-permute-start(bf16[1,2048,512]{2,1,0:T(8,128)(2,1)} %param.11), channel_id=1, source_target_pairs={{12,24},{13,25},{14,26},{15,27},{28,8},{29,9},{30,10},{31,11}} | collective-permute-start | bytes 6291464 | tf_op jit(solution)/shard_map/ppermute | solution.py:376
  19.3 4.7 %collective-permute-start.6 = (bf16[64,512]{1,0:T(8,128)(2,1)S(1)}, bf16[64,512]{1,0:T(8,128)(2,1)S(1)}, u32[]{:S(2)}, u32[]{:S(2)}) collective-permute-start(bf16[64,512]{1,0:T(8,128)(2,1)S(1)} %lookup.1.refs_1_), channel_id=1, source_target_pairs={{24,0},{9,1},{29,2},{12,3},{26,16},{11,17},{31,18},{14,19}} | collective-permute-start | bytes 196616 | tf_op jit(solution)/shard_map/ppermute | solution.py:376
  25.4 2.2 %copy-done = bf16[1,2048,1024]{2,1,0:T(8,128)(2,1)S(1)} copy-done((bf16[1,2048,1024]{2,1,0:T(8,128)(2,1)S(1)}, bf16[1,2048,1024]{2,1,0:T(8,128)(2,1)}, u32[]{:S(2)}) %copy-start) | copy-done | bytes 4194328
  27.7 1.4 %collective-permute-start.10 = (bf16[128,1152]{1,0:T(8,128)(2,1)S(1)}, bf16[128,1152]{1,0:T(8,128)(2,1)S(1)}, u32[]{:S(2)}, u32[]{:S(2)}) collective-permute-start(bf16[128,1152]{1,0:T(8,128)(2,1)S(1)} %get-tuple-element.31), channel_id=1, source_target_pairs={{0,4},{1,5},{2,6},{3,7},{16,20},{17,21},{18,22},{19,23},{8,12},{9,... | collective-permute-start | bytes 884744 | tf_op jit(solution)/shard_map/ppermute | solution.py:376
  31.3 9.4 %collective-permute-done.9.refs_0_ = bf16[128,1152]{1,0:T(8,128)(2,1)S(1)} collective-permute-done((bf16[128,1152]{1,0:T(8,128)(2,1)S(1)}, bf16[128,1152]{1,0:T(8,128)(2,1)S(1)}, u32[]{:S(2)}, u32[]{:S(2)}) %collective-permute-start.9) | collective-permute-done | bytes 294944 | tf_op jit(solution)/shard_map/ppermute | solution.py:376
  42.8 1.3 collective-permute-start.15
  48.5 1.9 %collective-permute-done.19.refs_3_ = bf16[128,512]{1,0:T(8,128)(2,1)S(1)} collective-permute-done((bf16[128,512]{1,0:T(8,128)(2,1)S(1)}, bf16[128,512]{1,0:T(8,128)(2,1)S(1)}, u32[]{:S(2)}, u32[]{:S(2)}) %collective-permute-start.19) | collective-permute-done | bytes 131104 | tf_op jit(solution)/shard_map/ppermute | solution.py:376
  51.1 2.1 %collective-permute-start.21 = (bf16[128,1152]{1,0:T(8,128)(2,1)S(1)}, bf16[128,1152]{1,0:T(8,128)(2,1)S(1)}, u32[]{:S(2)}, u32[]{:S(2)}) collective-permute-start(bf16[128,1152]{1,0:T(8,128)(2,1)S(1)} %get-tuple-element.37), channel_id=1, source_target_pairs={{4,0},{5,1},{6,2},{7,3},{20,16},{21,17},{22,18},{23,19},{12,8},{13... | collective-permute-start | bytes 884744 | tf_op jit(solution)/shard_map/ppermute | solution.py:376
  57.7 1.9 %collective-permute-done.25.refs_3_ = bf16[128,512]{1,0:T(8,128)(2,1)S(1)} collective-permute-done((bf16[128,512]{1,0:T(8,128)(2,1)S(1)}, bf16[128,512]{1,0:T(8,128)(2,1)S(1)}, u32[]{:S(2)}, u32[]{:S(2)}) %collective-permute-start.25) | collective-permute-done | bytes 131104 | tf_op jit(solution)/shard_map/ppermute | solution.py:376
  65.9 30.9 %collective-permute-done.30.refs_0_ = bf16[128,1152]{1,0:T(8,128)(2,1)S(1)} collective-permute-done((bf16[128,1152]{1,0:T(8,128)(2,1)S(1)}, bf16[128,1152]{1,0:T(8,128)(2,1)S(1)}, u32[]{:S(2)}, u32[]{:S(2)}) %collective-permute-start.30) | collective-permute-done | bytes 294944 | tf_op jit(solution)/shard_map/ppermute | solution.py:376
  97.9 1.3 collective-permute-start.32
  99.2 1.3 collective-permute-start.33
  100.5 1.3 collective-permute-start.34
  101.8 1.5 %collective-permute-start.35 = (bf16[128,512]{1,0:T(8,128)(2,1)S(1)}, bf16[128,512]{1,0:T(8,128)(2,1)S(1)}, u32[]{:S(2)}, u32[]{:S(2)}) collective-permute-start(bf16[128,512]{1,0:T(8,128)(2,1)S(1)} %get-tuple-element.47), channel_id=1, source_target_pairs={{4,0},{5,1},{6,2},{7,3},{20,16},{21,17},{22,18},{23,19},{12,8},{13... | collective-permute-start | bytes 393224 | tf_op jit(solution)/shard_map/ppermute | solution.py:376
  109.4 2.2 %copy-done.2 = bf16[1,2048,1024]{2,1,0:T(8,128)(2,1)S(1)} copy-done((bf16[1,2048,1024]{2,1,0:T(8,128)(2,1)S(1)}, bf16[1,2048,1024]{2,1,0:T(8,128)(2,1)}, u32[]{:S(2)}) %copy-start.2) | copy-done | bytes 4194328
  111.9 2.5 %collective-permute-done.37.refs_1_ = bf16[128,512]{1,0:T(8,128)(2,1)S(1)} collective-permute-done((bf16[128,512]{1,0:T(8,128)(2,1)S(1)}, bf16[128,512]{1,0:T(8,128)(2,1)S(1)}, u32[]{:S(2)}, u32[]{:S(2)}) %collective-permute-start.37) | collective-permute-done | bytes 131104 | tf_op jit(solution)/shard_map/ppermute | solution.py:376
  116.1 2.7 %collective-permute-start.47 = (bf16[64,1024]{1,0:T(8,128)(2,1)S(1)}, bf16[64,1024]{1,0:T(8,128)(2,1)S(1)}, u32[]{:S(2)}, u32[]{:S(2)}) collective-permute-start(bf16[64,1024]{1,0:T(8,128)(2,1)S(1)} %get-tuple-element.55), channel_id=1, source_target_pairs={{12,28},{13,29},{30,14},{31,15}} | collective-permute-start | bytes 393224 | tf_op jit(solution)/shard_map/ppermute | solution.py:376
  118.8 1.3 collective-permute-start.40
  120.1 1.3 collective-permute-start.41
  122.9 1.4 %collective-permute-start.48 = (bf16[64,1024]{1,0:T(8,128)(2,1)S(1)}, bf16[64,1024]{1,0:T(8,128)(2,1)S(1)}, u32[]{:S(2)}, u32[]{:S(2)}) collective-permute-start(bf16[64,1024]{1,0:T(8,128)(2,1)S(1)} %broadcast_select_fusion.refs_4_), channel_id=1, source_target_pairs={{4,0},{5,1},{6,2},{7,3},{20,16},{21,17},{22,18},{23,19},{12,8},{13... | collective-permute-start | bytes 393224 | tf_op jit(solution)/shard_map/ppermute | solution.py:376
  129.7 5.7 %collective-permute-done.43.refs_0_ = bf16[64,1024]{1,0:T(8,128)(2,1)S(1)} collective-permute-done((bf16[64,1024]{1,0:T(8,128)(2,1)S(1)}, bf16[64,1024]{1,0:T(8,128)(2,1)S(1)}, u32[]{:S(2)}, u32[]{:S(2)}) %collective-permute-start.43) | collective-permute-done | bytes 131104 | tf_op jit(solution)/shard_map/ppermute | solution.py:376
  (117 shorter events, 43.4 us)
Async XLA Ops:
  0.0 30.4 %collective-permute-start.11 = (bf16[1,2048,512]{2,1,0:T(8,128)(2,1)}, bf16[1,2048,512]{2,1,0:T(8,128)(2,1)S(1)}, u32[]{:S(2)}, u32[]{:S(2)}) collective-permute-start(bf16[1,2048,512]{2,1,0:T(8,128)(2,1)} %param.11), channel_id=1, source_target_pairs={{0,4},{4,0},{8,12},{12,8},{1,5},{5,1},{9,13},{13,9},{2,6},{6,2},{1... | collective-permute-start | bytes 6291464 | tf_op jit(solution)/shard_map/ppermute | solution.py:386
  12.4 7.0 %collective-permute-start.3 = (bf16[64,512]{1,0:T(8,128)(2,1)S(1)}, bf16[64,512]{1,0:T(8,128)(2,1)S(1)}, u32[]{:S(2)}, u32[]{:S(2)}) collective-permute-start(bf16[64,512]{1,0:T(8,128)(2,1)S(1)} %lookup.1.refs_1_), channel_id=1, source_target_pairs={{21,0},{4,1},{20,2},{5,3},{23,16},{6,17},{22,18},{7,19}} | collective-permute-start | bytes 196616 | tf_op jit(solution)/shard_map/ppermute | solution.py:376
  13.0 11.0 %collective-permute-start.4 = (bf16[64,512]{1,0:T(8,128)(2,1)S(1)}, bf16[64,512]{1,0:T(8,128)(2,1)S(1)}, u32[]{:S(2)}, u32[]{:S(2)}) collective-permute-start(bf16[64,512]{1,0:T(8,128)(2,1)S(1)} %lookup.1.refs_1_), channel_id=1, source_target_pairs={{25,0},{8,1},{28,2},{13,3},{27,16},{10,17},{30,18},{15,19}} | collective-permute-start | bytes 196616 | tf_op jit(solution)/shard_map/ppermute | solution.py:376
  13.7 11.0 %collective-permute-start.5 = (bf16[64,512]{1,0:T(8,128)(2,1)S(1)}, bf16[64,512]{1,0:T(8,128)(2,1)S(1)}, u32[]{:S(2)}, u32[]{:S(2)}) collective-permute-start(bf16[64,512]{1,0:T(8,128)(2,1)S(1)} %lookup.1.refs_1_), channel_id=1, source_target_pairs={{20,0},{5,1},{21,2},{4,3},{22,16},{7,17},{23,18},{6,19}} | collective-permute-start | bytes 196616 | tf_op jit(solution)/shard_map/ppermute | solution.py:376
  14.4 107.8 %collective-permute-start.42 = (bf16[1,2048,512]{2,1,0:T(8,128)(2,1)}, bf16[1,2048,512]{2,1,0:T(8,128)(2,1)}, u32[]{:S(2)}, u32[]{:S(2)}) collective-permute-start(bf16[1,2048,512]{2,1,0:T(8,128)(2,1)} %param.11), channel_id=1, source_target_pairs={{12,24},{13,25},{14,26},{15,27},{28,8},{29,9},{30,10},{31,11}} | collective-permute-start | bytes 6291464 | tf_op jit(solution)/shard_map/ppermute | solution.py:376
  19.3 8.3 %collective-permute-start.6 = (bf16[64,512]{1,0:T(8,128)(2,1)S(1)}, bf16[64,512]{1,0:T(8,128)(2,1)S(1)}, u32[]{:S(2)}, u32[]{:S(2)}) collective-permute-start(bf16[64,512]{1,0:T(8,128)(2,1)S(1)} %lookup.1.refs_1_), channel_id=1, source_target_pairs={{24,0},{9,1},{29,2},{12,3},{26,16},{11,17},{31,18},{14,19}} | collective-permute-start | bytes 196616 | tf_op jit(solution)/shard_map/ppermute | solution.py:376
  29.1 11.6 %collective-permute-start.9 = (bf16[128,1152]{1,0:T(8,128)(2,1)S(1)}, bf16[128,1152]{1,0:T(8,128)(2,1)S(1)}, u32[]{:S(2)}, u32[]{:S(2)}) collective-permute-start(bf16[128,1152]{1,0:T(8,128)(2,1)S(1)} %get-tuple-element.31), channel_id=1, source_target_pairs={{0,20},{1,21},{2,22},{3,23},{16,4},{17,5},{18,6},{19,7},{8,28},{9,... | collective-permute-start | bytes 884744 | tf_op jit(solution)/shard_map/ppermute | solution.py:376
  62.5 34.3 %collective-permute-start.30 = (bf16[128,1152]{1,0:T(8,128)(2,1)S(1)}, bf16[128,1152]{1,0:T(8,128)(2,1)S(1)}, u32[]{:S(2)}, u32[]{:S(2)}) collective-permute-start(bf16[128,1152]{1,0:T(8,128)(2,1)S(1)} %get-tuple-element.43), channel_id=1, source_target_pairs={{0,20},{1,21},{2,22},{3,23},{16,4},{17,5},{18,6},{19,7},{8,28},{9,... | collective-permute-start | bytes 884744 | tf_op jit(solution)/shard_map/ppermute | solution.py:376
  63.8 33.0 %collective-permute-start.31 = (bf16[128,1152]{1,0:T(8,128)(2,1)S(1)}, bf16[128,1152]{1,0:T(8,128)(2,1)S(1)}, u32[]{:S(2)}, u32[]{:S(2)}) collective-permute-start(bf16[128,1152]{1,0:T(8,128)(2,1)S(1)} %get-tuple-element.43), channel_id=1, source_target_pairs={{0,4},{1,5},{2,6},{3,7},{16,20},{17,21},{18,22},{19,23},{8,12},{9,... | collective-permute-start | bytes 884744 | tf_op jit(solution)/shard_map/ppermute | solution.py:376
  97.9 5.4 %collective-permute-start.32 = (bf16[128,512]{1,0:T(8,128)(2,1)S(1)}, bf16[128,512]{1,0:T(8,128)(2,1)S(1)}, u32[]{:S(2)}, u32[]{:S(2)}) collective-permute-start(bf16[128,512]{1,0:T(8,128)(2,1)S(1)} %get-tuple-element.44), channel_id=1, source_target_pairs={{12,10},{13,11},{14,8},{15,9},{28,26},{29,27},{30,24},{31,25}} | collective-permute-start | bytes 393224 | tf_op jit(solution)/shard_map/ppermute | solution.py:376
  104.2 7.7 %collective-permute-start.36 = (bf16[128,512]{1,0:T(8,128)(2,1)S(1)}, bf16[128,512]{1,0:T(8,128)(2,1)S(1)}, u32[]{:S(2)}, u32[]{:S(2)}) collective-permute-start(bf16[128,512]{1,0:T(8,128)(2,1)S(1)} %combine.5.refs_1_), channel_id=1, source_target_pairs={{8,14},{9,15},{10,12},{11,13},{24,30},{25,31},{26,28},{27,29}} | collective-permute-start | bytes 393224 | tf_op jit(solution)/shard_map/ppermute | solution.py:376
  105.5 8.9 %collective-permute-start.37 = (bf16[128,512]{1,0:T(8,128)(2,1)S(1)}, bf16[128,512]{1,0:T(8,128)(2,1)S(1)}, u32[]{:S(2)}, u32[]{:S(2)}) collective-permute-start(bf16[128,512]{1,0:T(8,128)(2,1)S(1)} %combine.5.refs_1_), channel_id=1, source_target_pairs={{8,13},{9,14},{10,15},{11,12},{24,29},{25,30},{26,31},{27,28}} | collective-permute-start | bytes 393224 | tf_op jit(solution)/shard_map/ppermute | solution.py:376
  106.8 8.5 %collective-permute-start.38 = (bf16[128,512]{1,0:T(8,128)(2,1)S(1)}, bf16[128,512]{1,0:T(8,128)(2,1)S(1)}, u32[]{:S(2)}, u32[]{:S(2)}) collective-permute-start(bf16[128,512]{1,0:T(8,128)(2,1)S(1)} %combine.5.refs_1_), channel_id=1, source_target_pairs={{8,15},{9,12},{10,13},{11,14},{24,31},{25,28},{26,29},{27,30}} | collective-permute-start | bytes 393224 | tf_op jit(solution)/shard_map/ppermute | solution.py:376
  108.1 7.2 %collective-permute-start.39 = (bf16[128,512]{1,0:T(8,128)(2,1)S(1)}, bf16[128,512]{1,0:T(8,128)(2,1)S(1)}, u32[]{:S(2)}, u32[]{:S(2)}) collective-permute-start(bf16[128,512]{1,0:T(8,128)(2,1)S(1)} %combine.5.refs_1_), channel_id=1, source_target_pairs={{0,4},{1,5},{2,6},{3,7},{16,20},{17,21},{18,22},{19,23},{8,12},{9,... | collective-permute-start | bytes 393224 | tf_op jit(solution)/shard_map/ppermute | solution.py:376
  116.1 6.8 %collective-permute-start.47 = (bf16[64,1024]{1,0:T(8,128)(2,1)S(1)}, bf16[64,1024]{1,0:T(8,128)(2,1)S(1)}, u32[]{:S(2)}, u32[]{:S(2)}) collective-permute-start(bf16[64,1024]{1,0:T(8,128)(2,1)S(1)} %get-tuple-element.55), channel_id=1, source_target_pairs={{12,28},{13,29},{30,14},{31,15}} | collective-permute-start | bytes 393224 | tf_op jit(solution)/shard_map/ppermute | solution.py:376
  118.8 5.6 %collective-permute-start.40 = (bf16[128,1152]{1,0:T(8,128)(2,1)S(1)}, bf16[128,1152]{1,0:T(8,128)(2,1)S(1)}, u32[]{:S(2)}, u32[]{:S(2)}) collective-permute-start(bf16[128,1152]{1,0:T(8,128)(2,1)S(1)} %get-tuple-element.49), channel_id=1, source_target_pairs={{12,24},{13,25},{14,26},{15,27},{28,8},{29,9},{30,10},{31,11}} | collective-permute-start | bytes 884744 | tf_op jit(solution)/shard_map/ppermute | solution.py:376
  120.1 4.2 %collective-permute-start.41 = (bf16[128,1152]{1,0:T(8,128)(2,1)S(1)}, bf16[128,1152]{1,0:T(8,128)(2,1)S(1)}, u32[]{:S(2)}, u32[]{:S(2)}) collective-permute-start(bf16[128,1152]{1,0:T(8,128)(2,1)S(1)} %get-tuple-element.49), channel_id=1, source_target_pairs={{4,0},{5,1},{6,2},{7,3},{20,16},{21,17},{22,18},{23,19},{12,8},{13... | collective-permute-start | bytes 884744 | tf_op jit(solution)/shard_map/ppermute | solution.py:376
  121.5 5.5 %collective-permute-start.49 = (bf16[64,512]{1,0:T(8,128)(2,1)S(1)}, bf16[64,512]{1,0:T(8,128)(2,1)S(1)}, u32[]{:S(2)}, u32[]{:S(2)}) collective-permute-start(bf16[64,512]{1,0:T(8,128)(2,1)S(1)} %get-tuple-element.58), channel_id=1, source_target_pairs={{0,0},{1,16},{2,1},{3,17},{16,2},{17,18},{18,3},{19,19},{4,4},{5,2... | collective-permute-start | bytes 196616 | tf_op jit(solution)/shard_map/ppermute | solution.py:376
  122.2 6.1 %collective-permute-start.50 = (bf16[64,512]{1,0:T(8,128)(2,1)S(1)}, bf16[64,512]{1,0:T(8,128)(2,1)S(1)}, u32[]{:S(2)}, u32[]{:S(2)}) collective-permute-start(bf16[64,512]{1,0:T(8,128)(2,1)S(1)} %get-tuple-element.57), channel_id=1, source_target_pairs={{0,16},{1,0},{2,17},{3,1},{16,18},{17,2},{18,19},{19,3},{4,20},{5,... | collective-permute-start | bytes 196616 | tf_op jit(solution)/shard_map/ppermute | solution.py:376
  122.9 6.7 %collective-permute-start.48 = (bf16[64,1024]{1,0:T(8,128)(2,1)S(1)}, bf16[64,1024]{1,0:T(8,128)(2,1)S(1)}, u32[]{:S(2)}, u32[]{:S(2)}) collective-permute-start(bf16[64,1024]{1,0:T(8,128)(2,1)S(1)} %broadcast_select_fusion.refs_4_), channel_id=1, source_target_pairs={{4,0},{5,1},{6,2},{7,3},{20,16},{21,17},{22,18},{23,19},{12,8},{13... | collective-permute-start | bytes 393224 | tf_op jit(solution)/shard_map/ppermute | solution.py:376
  124.4 10.9 %collective-permute-start.43 = (bf16[64,1024]{1,0:T(8,128)(2,1)S(1)}, bf16[64,1024]{1,0:T(8,128)(2,1)S(1)}, u32[]{:S(2)}, u32[]{:S(2)}) collective-permute-start(bf16[64,1024]{1,0:T(8,128)(2,1)S(1)} %get-tuple-element.50), channel_id=1, source_target_pairs={{8,14},{9,15},{10,12},{11,13},{24,30},{25,31},{26,28},{27,29}} | collective-permute-start | bytes 393224 | tf_op jit(solution)/shard_map/ppermute | solution.py:376
  125.7 9.6 %collective-permute-start.44 = (bf16[64,1024]{1,0:T(8,128)(2,1)S(1)}, bf16[64,1024]{1,0:T(8,128)(2,1)S(1)}, u32[]{:S(2)}, u32[]{:S(2)}) collective-permute-start(bf16[64,1024]{1,0:T(8,128)(2,1)S(1)} %get-tuple-element.51), channel_id=1, source_target_pairs={{8,13},{9,14},{10,15},{11,12},{24,29},{25,30},{26,31},{27,28}} | collective-permute-start | bytes 393224 | tf_op jit(solution)/shard_map/ppermute | solution.py:376
  127.0 9.3 %collective-permute-start.45 = (bf16[64,1024]{1,0:T(8,128)(2,1)S(1)}, bf16[64,1024]{1,0:T(8,128)(2,1)S(1)}, u32[]{:S(2)}, u32[]{:S(2)}) collective-permute-start(bf16[64,1024]{1,0:T(8,128)(2,1)S(1)} %get-tuple-element.52), channel_id=1, source_target_pairs={{8,15},{9,12},{10,13},{11,14},{24,31},{25,28},{26,29},{27,30}} | collective-permute-start | bytes 393224 | tf_op jit(solution)/shard_map/ppermute | solution.py:376
  128.3 8.0 %collective-permute-start.46 = (bf16[64,1024]{1,0:T(8,128)(2,1)S(1)}, bf16[64,1024]{1,0:T(8,128)(2,1)S(1)}, u32[]{:S(2)}, u32[]{:S(2)}) collective-permute-start(bf16[64,1024]{1,0:T(8,128)(2,1)S(1)} %get-tuple-element.53), channel_id=1, source_target_pairs={{0,4},{1,5},{2,6},{3,7},{16,20},{17,21},{18,22},{19,23},{8,12},{9,... | collective-permute-start | bytes 393224 | tf_op jit(solution)/shard_map/ppermute | solution.py:376
  (33 other events, 145.7 us)
